TPU v7x, 32 devices: a whole 2x2x4 slice. The times are simulated.
32 devices in a mesh: gx: 4 (over z), gy: 4 (over x, core), gz: 2 (over y).
Axes of the slice: x: 2, y: 2, z: 4, core: 2. Of those that a mesh axis runs over, the one named last changes fastest.
Arguments:
- offset: float32 [3, 32, 32, 256], P(None, 'gx', 'gy', 'gz'), may hold values from -0.25 to 0.25
- velocity: float32 [3, 32, 32, 256], P(None, 'gx', 'gy', 'gz'), may hold values from -3 to 3
- spin: float32 [3, 32, 32, 256], P(None, 'gx', 'gy', 'gz'), may hold values from -3 to 3
- radius: float32 [32, 32, 256], P('gx', 'gy', 'gz'), may hold values from 0.62 to 0.82
- history: float32 [6, 3, 32, 32, 256], P(None, None, 'gx', 'gy', 'gz'), may hold values from -0.3 to 0.3
- contacts: int32 [6, 32, 32, 256], P(None, 'gx', 'gy', 'gz'), may hold values from -1 to 8, as said below
- leaving: int32 [4, 4, 2, 64], P('gx', 'gy', 'gz'), may hold values from -1 to 8191, as said below
Outputs:
- new_offset: float32 [3, 32, 32, 256], P(None, 'gx', 'gy', 'gz')
- new_velocity: float32 [3, 32, 32, 256], P(None, 'gx', 'gy', 'gz')
- new_spin: float32 [3, 32, 32, 256], P(None, 'gx', 'gy', 'gz')
- new_history: float32 [6, 3, 32, 32, 256], P(None, None, 'gx', 'gy', 'gz')
- arrivals: float32 [28, 4, 4, 2, 64], P(None, 'gx', 'gy', 'gz')
Inputs may be any that keep to these rules, and one draw needn't show every extreme that they name: `contacts`: the live codes of one particle are distinct. `leaving`: each block's live entries are distinct cells with z index 0 or 1 within the block, listed first and followed by -1; at most 64 are live, and some block has 64 live.
All inputs are finite; a program needn't handle non-finite values.
Results may differ from a plain program's by a relative error of at most 0.0003.
Values sent between devices are 32-bit elements; how exact they have to be, the bound alone decides.
A program may use at most 512 MiB of HBM per device.

v0:
```python
import jax
import jax.numpy as jnp
from jax import lax
from jax.sharding import PartitionSpec as P

forward_dirs = [
    [1, 0, 0],
    [0, 1, 0],
    [0, 0, 1],
    [1, 1, 0],
    [1, -1, 0],
    [1, 0, 1],
    [1, 0, -1],
    [0, 1, 1],
    [0, 1, -1],
]
stiff_normal = 10.0
damp_normal = 2.0
stiff_shear = 8.0
damp_shear = 1.5
friction = 0.4
shear_floor = 0.05
time_step = 0.05
gravity = 1.0


def padded_2(cells, sides, width):
    for axis, dim in sides:
        count = lax.axis_size(axis)
        ends = count - 1
        head = lax.slice_in_dim(cells, 0, width, axis=dim)
        tail = lax.slice_in_dim(cells, cells.shape[dim] - width, cells.shape[dim], axis=dim)
        cells = jnp.concatenate(
            [
                lax.ppermute(tail, axis, [(i, (i + 1) % count) for i in range(ends)]),
                cells,
                lax.ppermute(head, axis, [((i + 1) % count, i) for i in range(ends)]),
            ],
            axis=dim,
        )
    return cells


def from_behind(block, axis, distance):
    devices = range(lax.axis_size(axis))
    route = [(i - distance, i) for i in devices if i - distance in devices]
    return lax.ppermute(block, axis, route)


def cross_product(first_vec, second_vec):
    return jnp.stack(
        [
            first_vec[1] * second_vec[2] - first_vec[2] * second_vec[1],
            first_vec[2] * second_vec[0] - first_vec[0] * second_vec[2],
            first_vec[0] * second_vec[1] - first_vec[1] * second_vec[0],
        ],
        0,
    )


def contact_pair(centers, partner, direction, shear):
    separation = direction + partner[0:3] - centers[0:3]
    distance = jnp.sqrt(jnp.sum(separation * separation, 0))
    normal = separation / distance
    radius_center = centers[9]
    radius_partner = partner[9]
    radius_sum = radius_center + radius_partner
    intersection = jnp.maximum(radius_sum - distance, 0.0)
    contact = jnp.sqrt(radius_center * radius_partner / radius_sum * intersection)
    relative = (
        partner[3:6]
        - centers[3:6]
        - cross_product(radius_center * centers[6:9] + radius_partner * partner[6:9], normal)
    )
    approach = jnp.sum(relative * normal, 0)
    sliding = relative - approach * normal
    repulsion = jnp.maximum(
        stiff_normal * contact * intersection - damp_normal * contact * approach, 0.0
    )
    spring = shear - jnp.sum(shear * normal, 0) * normal + time_step * sliding
    trial_force = stiff_shear * contact * spring + damp_shear * contact * sliding
    magnitude = jnp.sqrt(jnp.sum(trial_force * trial_force, 0))
    factor = jnp.minimum(1.0, friction * repulsion / jnp.maximum(magnitude, shear_floor))
    tangent = factor * trial_force
    pair_force = tangent - repulsion * normal
    twisting = cross_product(normal, tangent)
    return (pair_force, radius_center * twisting, radius_partner * twisting, factor * spring)


def contact_terms(centers, shear, codes, source, margin):
    count_x, count_y, count_z = centers.shape[1:]
    channels = source.shape[0]
    windows = []
    for step_dir in forward_dirs:
        begin = (0, margin + step_dir[0], margin + step_dir[1], margin + step_dir[2])
        finish = (channels, begin[1] + count_x, begin[2] + count_y, begin[3] + count_z)
        windows.append((begin, lax.slice(source, begin, finish)))
    own_terms = jnp.zeros((6, count_x, count_y, count_z), jnp.float32)
    per_dir = [jnp.zeros((6, count_x, count_y, count_z), jnp.float32) for step_dir in forward_dirs]
    springs = []
    for which_slot in range(codes.shape[0]):
        slot_code = codes[which_slot]
        slot_live = slot_code >= 0
        chosen = jnp.maximum(slot_code, 0)
        partner = jnp.zeros((channels, count_x, count_y, count_z), jnp.float32)
        direction = jnp.zeros((3, count_x, count_y, count_z), jnp.float32)
        for number, step_dir in enumerate(forward_dirs):
            picked_here = (chosen == number)[None]
            partner = partner + jnp.where(picked_here, windows[number][1], 0.0)
            direction = direction + jnp.where(
                picked_here, jnp.asarray(step_dir, jnp.float32).reshape(3, 1, 1, 1), 0.0
            )
        pair_force, torque_center, torque_partner, spring = contact_pair(
            centers, partner, direction, shear[which_slot]
        )
        own_terms = own_terms + jnp.where(
            slot_live[None], jnp.concatenate([pair_force, torque_center], 0), 0.0
        )
        reaction = jnp.where(
            slot_live[None], jnp.concatenate([-pair_force, torque_partner], 0), 0.0
        )
        for number in range(len(forward_dirs)):
            per_dir[number] = per_dir[number] + jnp.where((chosen == number)[None], reaction, 0.0)
        springs.append(jnp.where(slot_live[None], spring, 0.0))
    partner_terms = jnp.zeros((6,) + source.shape[1:], jnp.float32)
    for number in range(len(forward_dirs)):
        begin = windows[number][0]
        widths = (
            (0, 0),
            (begin[1], source.shape[1] - begin[1] - count_x),
            (begin[2], source.shape[2] - begin[2] - count_y),
            (begin[3], source.shape[3] - begin[3] - count_z),
        )
        partner_terms = partner_terms + jnp.pad(per_dir[number], widths)
    return (own_terms, partner_terms, jnp.stack(springs, 0))


def fold_rims(extended, axis_dim):
    length = extended.shape[axis_dim]
    middle = lax.slice_in_dim(extended, 2, length - 2, axis=axis_dim)
    lower = lax.slice_in_dim(extended, 0, 1, axis=axis_dim)
    upper = lax.slice_in_dim(extended, length - 1, length, axis=axis_dim)
    inner = middle.shape[axis_dim]
    return jnp.concatenate(
        [
            lax.slice_in_dim(middle, 0, 1, axis=axis_dim) + lower,
            lax.slice_in_dim(middle, 1, inner - 1, axis=axis_dim),
            lax.slice_in_dim(middle, inner - 1, inner, axis=axis_dim) + upper,
        ],
        axis_dim,
    )


def on_device(offset, velocity, spin, radius, history, contacts, leaving):
    cells_x, cells_y, cells_z = radius.shape
    slot_count = contacts.shape[0]
    fields = jnp.concatenate([offset, velocity, spin, radius[None]], 0)
    padded = padded_2(fields, (("gx", 1), ("gy", 2), ("gz", 3)), 1)
    own_terms, partner_terms, springs = contact_terms(fields, history, contacts, padded, 1)
    extended = padded_2(partner_terms, (("gx", 1), ("gy", 2), ("gz", 3)), 1)
    returned = fold_rims(fold_rims(fold_rims(extended, 1), 2), 3)
    totals = own_terms + returned
    particle_mass = radius**3
    downward = jnp.asarray([0.0, 0.0, -gravity], dtype=jnp.float32).reshape(3, 1, 1, 1)
    moved_velocity = velocity + time_step * (totals[0:3] / particle_mass + downward)
    moved_spin = spin + time_step * totals[3:6] / (0.4 * particle_mass * radius * radius)
    moved_offset = offset + time_step * moved_velocity
    bottom_shape = (cells_x, cells_y, 2)
    coord_x = jnp.broadcast_to(
        (lax.axis_index("gx") * cells_x + jnp.arange(cells_x, dtype=jnp.int32)).astype(jnp.float32)[
            :, None, None
        ],
        bottom_shape,
    )
    coord_y = jnp.broadcast_to(
        (lax.axis_index("gy") * cells_y + jnp.arange(cells_y, dtype=jnp.int32)).astype(jnp.float32)[
            None, :, None
        ],
        bottom_shape,
    )
    coord_z = jnp.broadcast_to(
        (lax.axis_index("gz") * cells_z + jnp.arange(2, dtype=jnp.int32)).astype(jnp.float32)[
            None, None, :
        ],
        bottom_shape,
    )
    bottom_position = jnp.stack([coord_x, coord_y, coord_z], 0) + moved_offset[:, :, :, 0:2]
    bottom_count = cells_x * cells_y * 2
    pieces = [
        bottom_position,
        moved_velocity[:, :, :, 0:2],
        moved_spin[:, :, :, 0:2],
        radius[None, :, :, 0:2],
        springs[:, :, :, :, 0:2].reshape(3 * slot_count, cells_x, cells_y, 2),
    ]
    bottom_rows = jnp.concatenate(
        [piece.reshape(piece.shape[0], bottom_count) for piece in pieces], 0
    )
    leave_index = leaving.reshape(-1)
    leave_live = leave_index >= 0
    picked = jnp.maximum(leave_index, 0)
    candidate = picked // cells_z * 2 + picked % cells_z
    selector = jnp.logical_and(
        jnp.arange(bottom_count, dtype=jnp.int32)[:, None] == candidate[None, :],
        leave_live[None, :],
    ).astype(jnp.float32)
    outbox = jnp.dot(
        bottom_rows, selector, precision=lax.Precision.HIGHEST, preferred_element_type=jnp.float32
    )
    arrivals = from_behind(outbox, "gz", -1)
    arrivals = arrivals.reshape(outbox.shape[0], 1, 1, 1, outbox.shape[1])
    departed = jnp.sum(selector, 1).reshape(cells_x, cells_y, 2)
    staying = jnp.concatenate(
        [1.0 - departed, jnp.ones((cells_x, cells_y, cells_z - 2), jnp.float32)], 2
    )
    return (
        moved_offset * staying,
        moved_velocity * staying,
        moved_spin * staying,
        springs * staying,
        arrivals,
    )


def solution(mesh):
    placed = (
        P(None, "gx", "gy", "gz"),
        P(None, "gx", "gy", "gz"),
        P(None, "gx", "gy", "gz"),
        P("gx", "gy", "gz"),
        P(None, None, "gx", "gy", "gz"),
        P(None, "gx", "gy", "gz"),
        P("gx", "gy", "gz", None),
    )
    return jax.shard_map(
        on_device,
        mesh=mesh,
        in_specs=placed,
        out_specs=(
            P(None, "gx", "gy", "gz"),
            P(None, "gx", "gy", "gz"),
            P(None, "gx", "gy", "gz"),
            P(None, None, "gx", "gy", "gz"),
            P(None, "gx", "gy", "gz", None),
        ),
        check_vma=False,
    )
```

profile of v0, /device:TPU:0, one launch (start us, length us, event | category | flops | bytes accessed | tf_op | source)
XLA Modules:
  0.0 112.1 jit_solution(6221109752881211208)
XLA Ops:
  0.7 0.9 pad_maximum_fusion.38
  1.5 1.3 %collective-permute-start = (f32[10,1,8,128]{3,2,1,0:T(8,128)S(1)}, f32[10,1,8,128]{3,2,1,0:T(8,128)S(1)}, u32[]{:S(2)}, u32[]{:S(2)}) collective-permute-start(f32[10,1,8,128]{3,2,1,0:T(8,128)S(1)} %get-tuple-element.147), channel_id=1, source_target_pairs={{8,0},{16,8},{24,16},{9,1},{17,9},{25,17},{10,2},{18,10},{26,18},{... | collective-permute-start | bytes 122888 | tf_op jit(solution)/shard_map/ppermute | solution.py:37
  2.8 5.6 %collective-permute-start.1 = (f32[10,1,8,128]{3,2,1,0:T(8,128)S(1)}, f32[10,1,8,128]{3,2,1,0:T(8,128)S(1)}, u32[]{:S(2)}, u32[]{:S(2)}) collective-permute-start(f32[10,1,8,128]{3,2,1,0:T(8,128)S(1)} %get-tuple-element.146), channel_id=1, source_target_pairs={{0,8},{8,16},{16,24},{1,9},{9,17},{17,25},{2,10},{10,18},{18,26},{... | collective-permute-start | bytes 122888 | tf_op jit(solution)/shard_map/ppermute | solution.py:35
  8.4 0.9 compare_bitcast_fusion.59
  9.5 1.5 %compare_bitcast_fusion.39 = (pred[8,8,128]{2,1,0:T(8,128)(4,1)S(1)}, pred[8,8,128]{2,1,0:T(8,128)(4,1)S(1)}, pred[8,8,128]{2,1,0:T(8,128)(4,1)S(1)}, pred[8,8,1...) fusion(s32[6,8,8,128]{3,2,1,0:T(8,128)} %param.67), kind=kLoop, calls=%fused_computation.333 | loop fusion | flops 204800 | bytes 352256 | tf_op jit(solution)/shard_map/jit(_where)/broadcast_in_dim | solution.py:116
  11.2 1.5 %compare_bitcast_fusion.49 = (pred[8,8,128]{2,1,0:T(8,128)(4,1)S(1)}, pred[8,8,128]{2,1,0:T(8,128)(4,1)}, pred[8,8,128]{2,1,0:T(8,128)(4,1)S(1)}, pred[8,8,128]{...) fusion(s32[6,8,8,128]{3,2,1,0:T(8,128)} %param.67), kind=kLoop, calls=%fused_computation.343 | loop fusion | flops 180224 | bytes 253952 | tf_op jit(solution)/shard_map/jit(_where)/broadcast_in_dim | solution.py:116
  13.6 1.1 %compare_bitcast_fusion.60 = pred[64]{0:T(512)(128)(4,1)} fusion(s32[1,1,1,64]{3,2,1,0:T(1,128)} %param.68), kind=kLoop, calls=%fused_computation.377 | loop fusion | flops 64 | bytes 320 | tf_op jit(solution)/shard_map/ge | solution.py:200
  14.7 1.2 %fusion.59 = s32[64]{0:T(128)} fusion(s32[1,1,1,64]{3,2,1,0:T(1,128)} %param.68), kind=kLoop, calls=%fused_computation.379 | loop fusion | flops 960 | bytes 512 | tf_op jit(solution)/shard_map/add | solution.py:202
  17.1 1.2 %pad_maximum_fusion.32 = (f32[10,10,1,128]{3,2,1,0:T(1,128)S(1)}, f32[10,10,1,128]{3,2,1,0:T(1,128)S(1)}) fusion(f32[10,1,8,128]{3,2,1,0:T(8,128)S(1)} %collective-permute-done, f32[10,1,8,128]{3,2,1,0:T(8,128)S(1)} %collective-permute-done.1, f32[1,8,8,128]{3,2,1,0:T(8,128)} %bitcast.285, f32[3,8,8,128]{3,2,1,0:T(8,128)} %param.64, ...), kind=kLoop, calls=%fused_computation.195 | loop fusion | flops 128000 | bytes 512000 | tf_op jit(solution)/shard_map/concatenate | solution.py:33
  18.4 1.3 %collective-permute-start.2 = (f32[10,10,1,128]{3,2,1,0:T(1,128)S(1)}, f32[10,10,1,128]{3,2,1,0:T(1,128)S(1)}, u32[]{:S(2)}, u32[]{:S(2)}) collective-permute-start(f32[10,10,1,128]{3,2,1,0:T(1,128)S(1)} %get-tuple-element.143), channel_id=1, source_target_pairs={{2,0},{4,2},{6,4},{3,1},{5,3},{7,5},{10,8},{12,10},{14,12},{11,9},... | collective-permute-start | bytes 153608 | tf_op jit(solution)/shard_map/ppermute | solution.py:37
  19.7 3.0 %collective-permute-start.3 = (f32[10,10,1,128]{3,2,1,0:T(1,128)S(1)}, f32[10,10,1,128]{3,2,1,0:T(1,128)S(1)}, u32[]{:S(2)}, u32[]{:S(2)}) collective-permute-start(f32[10,10,1,128]{3,2,1,0:T(1,128)S(1)} %get-tuple-element.142), channel_id=1, source_target_pairs={{0,2},{2,4},{4,6},{1,3},{3,5},{5,7},{8,10},{10,12},{12,14},{9,11},... | collective-permute-start | bytes 153608 | tf_op jit(solution)/shard_map/ppermute | solution.py:35
  22.7 0.8 collective-permute-done.3
  24.7 1.3 %collective-permute-start.4 = (f32[10,10,10,1]{2,3,1,0:T(1,128)S(1)}, f32[10,10,10,1]{2,3,1,0:T(1,128)S(1)}, u32[]{:S(2)}, u32[]{:S(2)}) collective-permute-start(f32[10,10,10,1]{2,3,1,0:T(1,128)S(1)} %copy.361), channel_id=1, source_target_pairs={{1,0},{3,2},{5,4},{7,6},{9,8},{11,10},{13,12},{15,14},{17,16},{19,... | collective-permute-start | bytes 12008 | tf_op jit(solution)/shard_map/ppermute | solution.py:37
  26.7 4.7 %collective-permute-start.5 = (f32[10,10,10,1]{2,3,1,0:T(1,128)S(1)}, f32[10,10,10,1]{2,3,1,0:T(1,128)S(1)}, u32[]{:S(2)}, u32[]{:S(2)}) collective-permute-start(f32[10,10,10,1]{2,3,1,0:T(1,128)S(1)} %copy.362), channel_id=1, source_target_pairs={{0,1},{2,3},{4,5},{6,7},{8,9},{10,11},{12,13},{14,15},{16,17},{18,... | collective-permute-start | bytes 12008 | tf_op jit(solution)/shard_map/ppermute | solution.py:35
  31.7 0.9 copy.356
  34.7 2.3 %pad_maximum_fusion = (f32[10,10,10,129]{3,2,1,0:T(8,128)S(1)}, f32[10,10,10,129]{3,2,1,0:T(8,128)S(1)}) fusion(f32[10,10,10,1]{3,2,1,0:T(8,128)S(1)} %copy.343, f32[10,10,1,128]{3,2,1,0:T(1,128)S(1)} %collective-permute-done.2, f32[10,1,8,128]{3,2,1,0:T(8,128)S(1)} %collective-permute-done, f32[1,8,8,128]{3,2,1,0:T(8,128)S(1)} %bitcast.288, ...), kind=kLoop, calls=%fused_computation | loop fusion | flops 2064000 | bytes 1552000 | tf_op jit(solution)/shard_map/concatenate | solution.py:33
  37.0 1.3 %select_add_fusion.1 = (f32[10,8,8,128]{3,2,1,0:T(8,128)S(1)}, f32[10,8,8,128]{3,2,1,0:T(8,128)S(1)}, f32[10,8,8,128]{3,2,1,0:T(8,128)S(1)}, f32[10,8,8,128]{3,2,1,0:T(8,128)S(1)}) fusion(f32[10,10,10,129]{3,2,1,0:T(8,128)S(1)} %get-tuple-element.141, f32[10,10,10,129]{3,2,1,0:T(8,128)S(1)} %get-tuple-element.140, ...), kind=kLoop, calls=%fused_computation.26 | loop fusion | flops 3194880 | bytes 3534848 | tf_op jit(solution)/shard_map/add | solution.py:109
  39.2 1.1 %select_add_fusion.4 = f32[10,8,8,128]{3,2,1,0:T(8,128)S(1)} fusion(f32[10,8,8,128]{3,2,1,0:T(8,128)S(1)} %get-tuple-element.113, f32[10,8,8,128]{3,2,1,0:T(8,128)S(1)} %get-tuple-element.112, f32[10,8,8,128]{3,2,1,0:T(8,128)S(1)} %get-tuple-element.111, f32[10,10,10,129]{3,2,1,0:T(8,128)S(1)} %get-tuple-element.141, ...), kind=kLoop, calls=%fused_computation.29 | loop fusion | flops 1720320 | bytes 3391488 | tf_op jit(solution)/shard_map/add | solution.py:109
  40.4 0.9 multiply_reduce_fusion.14
  41.4 1.2 %select_add_fusion.3 = f32[10,8,8,128]{3,2,1,0:T(8,128)S(1)} fusion(f32[10,8,8,128]{3,2,1,0:T(8,128)S(1)} %get-tuple-element.113, f32[10,8,8,128]{3,2,1,0:T(8,128)S(1)} %get-tuple-element.112, f32[10,8,8,128]{3,2,1,0:T(8,128)S(1)} %get-tuple-element.111, f32[10,10,10,129]{3,2,1,0:T(8,128)S(1)} %get-tuple-element.141, ...), kind=kLoop, calls=%fused_computation.28 | loop fusion | flops 1720320 | bytes 3391488 | tf_op jit(solution)/shard_map/add | solution.py:109
  42.6 0.9 multiply_reduce_fusion.11
  43.5 1.1 %select_add_fusion.2 = f32[10,8,8,128]{3,2,1,0:T(8,128)S(1)} fusion(f32[10,8,8,128]{3,2,1,0:T(8,128)S(1)} %get-tuple-element.113, f32[10,8,8,128]{3,2,1,0:T(8,128)S(1)} %get-tuple-element.112, f32[10,8,8,128]{3,2,1,0:T(8,128)S(1)} %get-tuple-element.111, f32[10,10,10,129]{3,2,1,0:T(8,128)S(1)} %get-tuple-element.141, ...), kind=kLoop, calls=%fused_computation.27 | loop fusion | flops 1720320 | bytes 3391488 | tf_op jit(solution)/shard_map/add | solution.py:109
  44.7 0.9 multiply_reduce_fusion.8
  45.6 1.1 select_add_fusion
  46.8 0.9 multiply_reduce_fusion.2
  47.8 0.9 multiply_reduce_fusion.5
  57.9 0.9 select_add_fusion.14
  58.9 0.9 select_add_fusion.13
  59.9 0.9 select_add_fusion.12
  60.9 0.9 select_add_fusion.11
  63.6 1.4 %pad_add_fusion = f32[6,10,10,130]{3,2,1,0:T(8,128)S(1)} fusion(f32[6,8,8,128]{3,2,1,0:T(8,128)S(1)} %select_add_fusion.6, f32[6,8,8,128]{3,2,1,0:T(8,128)S(1)} %select_add_fusion.7, f32[6,8,8,128]{3,2,1,0:T(8,128)S(1)} %select_add_fusion.8, f32[6,8,8,128]{3,2,1,0:T(8,128)S(1)} %select_add_fusion.9, f32[6,8,8,128]{3,2,1,0:T(8,128)S(1)} %select_add_fusion.10, ...), kind=kLoop, calls=%fused_computation.4 | loop fusion | flops 624000 | bytes 2081472 | tf_op jit(solution)/shard_map/add | solution.py:134
  65.1 3.9 %collective-permute-start.6 = (f32[6,1,10,130]{3,2,1,0:T(8,128)S(1)}, f32[6,1,10,130]{3,2,1,0:T(8,128)S(1)}, u32[]{:S(2)}, u32[]{:S(2)}) collective-permute-start(f32[6,1,10,130]{3,2,1,0:T(8,128)S(1)} %get-tuple-element.128), channel_id=1, source_target_pairs={{0,8},{8,16},{16,24},{1,9},{9,17},{17,25},{2,10},{10,18},{18,26},{... | collective-permute-start | bytes 93608 | tf_op jit(solution)/shard_map/ppermute | solution.py:35
  69.0 1.3 %collective-permute-start.7 = (f32[6,1,10,130]{3,2,1,0:T(8,128)S(1)}, f32[6,1,10,130]{3,2,1,0:T(8,128)S(1)}, u32[]{:S(2)}, u32[]{:S(2)}) collective-permute-start(f32[6,1,10,130]{3,2,1,0:T(8,128)S(1)} %get-tuple-element.129), channel_id=1, source_target_pairs={{8,0},{16,8},{24,16},{9,1},{17,9},{25,17},{10,2},{18,10},{26,18},{... | collective-permute-start | bytes 93608 | tf_op jit(solution)/shard_map/ppermute | solution.py:37
  70.4 1.7 %collective-permute-done.6 = f32[6,1,10,130]{3,2,1,0:T(8,128)S(1)} collective-permute-done((f32[6,1,10,130]{3,2,1,0:T(8,128)S(1)}, f32[6,1,10,130]{3,2,1,0:T(8,128)S(1)}, u32[]{:S(2)}, u32[]{:S(2)}) %collective-permute-start.6) | collective-permute-done | bytes 31232 | tf_op jit(solution)/shard_map/ppermute | solution.py:35
  72.1 4.1 %collective-permute-done.7 = f32[6,1,10,130]{3,2,1,0:T(8,128)S(1)} collective-permute-done((f32[6,1,10,130]{3,2,1,0:T(8,128)S(1)}, f32[6,1,10,130]{3,2,1,0:T(8,128)S(1)}, u32[]{:S(2)}, u32[]{:S(2)}) %collective-permute-start.7) | collective-permute-done | bytes 31232 | tf_op jit(solution)/shard_map/ppermute | solution.py:37
  76.3 1.6 %collective-permute-start.8 = (f32[6,12,1,130]{3,2,1,0:T(1,128)S(1)}, f32[6,12,1,130]{3,2,1,0:T(1,128)S(1)}, u32[]{:S(2)}, u32[]{:S(2)}) collective-permute-start(f32[6,12,1,130]{3,2,1,0:T(1,128)S(1)} %get-tuple-element.126), channel_id=1, source_target_pairs={{0,2},{2,4},{4,6},{1,3},{3,5},{5,7},{8,10},{10,12},{12,14},{9,11},... | collective-permute-start | bytes 112328 | tf_op jit(solution)/shard_map/ppermute | solution.py:35
  78.0 1.5 %collective-permute-start.9 = (f32[6,12,1,130]{3,2,1,0:T(1,128)S(1)}, f32[6,12,1,130]{3,2,1,0:T(1,128)S(1)}, u32[]{:S(2)}, u32[]{:S(2)}) collective-permute-start(f32[6,12,1,130]{3,2,1,0:T(1,128)S(1)} %get-tuple-element.127), channel_id=1, source_target_pairs={{2,0},{4,2},{6,4},{3,1},{5,3},{7,5},{10,8},{12,10},{14,12},{11,9},... | collective-permute-start | bytes 112328 | tf_op jit(solution)/shard_map/ppermute | solution.py:37
  79.5 4.5 %collective-permute-done.9 = f32[6,12,1,130]{3,2,1,0:T(1,128)S(1)} collective-permute-done((f32[6,12,1,130]{3,2,1,0:T(1,128)S(1)}, f32[6,12,1,130]{3,2,1,0:T(1,128)S(1)}, u32[]{:S(2)}, u32[]{:S(2)}) %collective-permute-start.9) | collective-permute-done | bytes 37472 | tf_op jit(solution)/shard_map/ppermute | solution.py:37
  84.3 1.2 %fusion.80 = (f32[6,12,12,1]{3,2,1,0:T(8,128)}, f32[6,12,12,1]{3,2,1,0:T(8,128)}) fusion(f32[6,12,12,130]{3,2,1,0:T(8,128)S(1)} %pad_maximum_fusion.1), kind=kLoop, calls=%fused_computation.390 | loop fusion | bytes 13824 | tf_op jit(solution)/shard_map/slice | solution.py:32
  85.5 1.6 %copy.346 = f32[6,12,12,1]{2,3,1,0:T(1,128)S(1)} copy(f32[6,12,12,1]{3,2,1,0:T(8,128)} %get-tuple-element.124) | data formatting | bytes 6912 | tf_op jit(solution)/shard_map/slice | solution.py:32
  87.1 3.3 %collective-permute-start.10 = (f32[6,12,12,1]{2,3,1,0:T(1,128)S(1)}, f32[6,12,12,1]{2,3,1,0:T(1,128)S(1)}, u32[]{:S(2)}, u32[]{:S(2)}) collective-permute-start(f32[6,12,12,1]{2,3,1,0:T(1,128)S(1)} %copy.346), channel_id=1, source_target_pairs={{0,1},{2,3},{4,5},{6,7},{8,9},{10,11},{12,13},{14,15},{16,17},{18,... | collective-permute-start | bytes 10376 | tf_op jit(solution)/shard_map/ppermute | solution.py:35
  90.4 1.6 %copy.347 = f32[6,12,12,1]{2,3,1,0:T(1,128)S(1)} copy(f32[6,12,12,1]{3,2,1,0:T(8,128)} %get-tuple-element.125) | data formatting | bytes 6912 | tf_op jit(solution)/shard_map/slice | solution.py:31
  92.0 1.3 %collective-permute-start.11 = (f32[6,12,12,1]{2,3,1,0:T(1,128)S(1)}, f32[6,12,12,1]{2,3,1,0:T(1,128)}, u32[]{:S(2)}, u32[]{:S(2)}) collective-permute-start(f32[6,12,12,1]{2,3,1,0:T(1,128)S(1)} %copy.347), channel_id=1, source_target_pairs={{1,0},{3,2},{5,4},{7,6},{9,8},{11,10},{13,12},{15,14},{17,16},{19,... | collective-permute-start | bytes 10376 | tf_op jit(solution)/shard_map/ppermute | solution.py:37
  94.2 3.7 %collective-permute-done.11 = f32[6,12,12,1]{2,3,1,0:T(1,128)} collective-permute-done((f32[6,12,12,1]{2,3,1,0:T(1,128)S(1)}, f32[6,12,12,1]{2,3,1,0:T(1,128)}, u32[]{:S(2)}, u32[]{:S(2)}) %collective-permute-start.11) | collective-permute-done | bytes 3488 | tf_op jit(solution)/shard_map/ppermute | solution.py:37
  97.9 1.3 %copy.349 = f32[6,12,12,1]{3,2,1,0:T(8,128)S(1)} copy(f32[6,12,12,1]{2,3,1,0:T(1,128)} %collective-permute-done.11) | data formatting | bytes 6912 | tf_op jit(solution)/shard_map/ppermute | solution.py:37
  105.8 1.3 %collective-permute-start.12 = (f32[28,64]{1,0:T(8,128)S(1)}, f32[28,64]{1,0:T(8,128)S(1)}, u32[]{:S(2)}, u32[]{:S(2)}) collective-permute-start(f32[28,64]{1,0:T(8,128)S(1)} %fusion.54), channel_id=1, source_target_pairs={{1,0},{3,2},{5,4},{7,6},{9,8},{11,10},{13,12},{15,14},{17,16},{19,... | collective-permute-start | bytes 21512 | tf_op jit(solution)/shard_map/ppermute | solution.py:47
  107.1 0.9 broadcast_multiply_fusion
  108.0 3.5 %collective-permute-done.12 = f32[28,64]{1,0:T(8,128)S(1)} collective-permute-done((f32[28,64]{1,0:T(8,128)S(1)}, f32[28,64]{1,0:T(8,128)S(1)}, u32[]{:S(2)}, u32[]{:S(2)}) %collective-permute-start.12) | collective-permute-done | bytes 7200 | tf_op jit(solution)/shard_map/ppermute | solution.py:47
  (341 shorter events, 26.3 us)
Async XLA Ops:
  1.5 15.6 %collective-permute-start = (f32[10,1,8,128]{3,2,1,0:T(8,128)S(1)}, f32[10,1,8,128]{3,2,1,0:T(8,128)S(1)}, u32[]{:S(2)}, u32[]{:S(2)}) collective-permute-start(f32[10,1,8,128]{3,2,1,0:T(8,128)S(1)} %get-tuple-element.147), channel_id=1, source_target_pairs={{8,0},{16,8},{24,16},{9,1},{17,9},{25,17},{10,2},{18,10},{26,18},{... | collective-permute-start | bytes 122888 | tf_op jit(solution)/shard_map/ppermute | solution.py:37
  2.8 14.3 %collective-permute-start.1 = (f32[10,1,8,128]{3,2,1,0:T(8,128)S(1)}, f32[10,1,8,128]{3,2,1,0:T(8,128)S(1)}, u32[]{:S(2)}, u32[]{:S(2)}) collective-permute-start(f32[10,1,8,128]{3,2,1,0:T(8,128)S(1)} %get-tuple-element.146), channel_id=1, source_target_pairs={{0,8},{8,16},{16,24},{1,9},{9,17},{17,25},{2,10},{10,18},{18,26},{... | collective-permute-start | bytes 122888 | tf_op jit(solution)/shard_map/ppermute | solution.py:35
  9.3 35.3 %copy-start.52 = (pred[8,8,128]{2,1,0:T(8,128)(4,1)}, pred[8,8,128]{2,1,0:T(8,128)(4,1)S(1)}, u32[]{:S(2)}) copy-start(pred[8,8,128]{2,1,0:T(8,128)(4,1)S(1)} %get-tuple-element.168) | copy-start | bytes 24580
  9.4 35.3 %copy-start.58 = (pred[8,8,128]{2,1,0:T(8,128)(4,1)}, pred[8,8,128]{2,1,0:T(8,128)(4,1)S(1)}, u32[]{:S(2)}) copy-start(pred[8,8,128]{2,1,0:T(8,128)(4,1)S(1)} %get-tuple-element.167) | copy-start | bytes 24580
  9.4 37.4 %copy-start.20 = (pred[8,8,128]{2,1,0:T(8,128)(4,1)}, pred[8,8,128]{2,1,0:T(8,128)(4,1)S(1)}, u32[]{:S(2)}) copy-start(pred[8,8,128]{2,1,0:T(8,128)(4,1)S(1)} %get-tuple-element.156) | copy-start | bytes 24580
  9.4 37.4 %copy-start.24 = (pred[8,8,128]{2,1,0:T(8,128)(4,1)}, pred[8,8,128]{2,1,0:T(8,128)(4,1)S(1)}, u32[]{:S(2)}) copy-start(pred[8,8,128]{2,1,0:T(8,128)(4,1)S(1)} %get-tuple-element.155) | copy-start | bytes 24580
  9.4 37.4 %copy-start.32 = (pred[8,8,128]{2,1,0:T(8,128)(4,1)}, pred[8,8,128]{2,1,0:T(8,128)(4,1)S(1)}, u32[]{:S(2)}) copy-start(pred[8,8,128]{2,1,0:T(8,128)(4,1)S(1)} %get-tuple-element.154) | copy-start | bytes 24580
  9.4 37.4 %copy-start.40 = (pred[8,8,128]{2,1,0:T(8,128)(4,1)}, pred[8,8,128]{2,1,0:T(8,128)(4,1)S(1)}, u32[]{:S(2)}) copy-start(pred[8,8,128]{2,1,0:T(8,128)(4,1)S(1)} %get-tuple-element.153) | copy-start | bytes 24580
  9.4 37.4 %copy-start.48 = (pred[8,8,128]{2,1,0:T(8,128)(4,1)}, pred[8,8,128]{2,1,0:T(8,128)(4,1)S(1)}, u32[]{:S(2)}) copy-start(pred[8,8,128]{2,1,0:T(8,128)(4,1)S(1)} %get-tuple-element.152) | copy-start | bytes 24580
  9.4 37.4 %copy-start.54 = (pred[8,8,128]{2,1,0:T(8,128)(4,1)}, pred[8,8,128]{2,1,0:T(8,128)(4,1)S(1)}, u32[]{:S(2)}) copy-start(pred[8,8,128]{2,1,0:T(8,128)(4,1)S(1)} %get-tuple-element.151) | copy-start | bytes 24580
  9.4 38.3 %copy-start.22 = (pred[8,8,128]{2,1,0:T(8,128)(4,1)}, pred[8,8,128]{2,1,0:T(8,128)(4,1)S(1)}, u32[]{:S(2)}) copy-start(pred[8,8,128]{2,1,0:T(8,128)(4,1)S(1)} %get-tuple-element.164) | copy-start | bytes 24580
  9.4 38.3 %copy-start.26 = (pred[8,8,128]{2,1,0:T(8,128)(4,1)}, pred[8,8,128]{2,1,0:T(8,128)(4,1)S(1)}, u32[]{:S(2)}) copy-start(pred[8,8,128]{2,1,0:T(8,128)(4,1)S(1)} %get-tuple-element.163) | copy-start | bytes 24580
  9.4 38.3 %copy-start.34 = (pred[8,8,128]{2,1,0:T(8,128)(4,1)}, pred[8,8,128]{2,1,0:T(8,128)(4,1)S(1)}, u32[]{:S(2)}) copy-start(pred[8,8,128]{2,1,0:T(8,128)(4,1)S(1)} %get-tuple-element.162) | copy-start | bytes 24580
  9.5 38.3 %copy-start.42 = (pred[8,8,128]{2,1,0:T(8,128)(4,1)}, pred[8,8,128]{2,1,0:T(8,128)(4,1)S(1)}, u32[]{:S(2)}) copy-start(pred[8,8,128]{2,1,0:T(8,128)(4,1)S(1)} %get-tuple-element.161) | copy-start | bytes 24580
  9.5 38.3 %copy-start.50 = (pred[8,8,128]{2,1,0:T(8,128)(4,1)}, pred[8,8,128]{2,1,0:T(8,128)(4,1)S(1)}, u32[]{:S(2)}) copy-start(pred[8,8,128]{2,1,0:T(8,128)(4,1)S(1)} %get-tuple-element.160) | copy-start | bytes 24580
  9.5 38.3 %copy-start.56 = (pred[8,8,128]{2,1,0:T(8,128)(4,1)}, pred[8,8,128]{2,1,0:T(8,128)(4,1)S(1)}, u32[]{:S(2)}) copy-start(pred[8,8,128]{2,1,0:T(8,128)(4,1)S(1)} %get-tuple-element.159) | copy-start | bytes 24580
  11.0 27.8 %copy-start.46 = (pred[8,8,128]{2,1,0:T(8,128)(4,1)}, pred[8,8,128]{2,1,0:T(8,128)(4,1)S(1)}, u32[]{:S(2)}) copy-start(pred[8,8,128]{2,1,0:T(8,128)(4,1)S(1)} %get-tuple-element.198) | copy-start | bytes 24580
  11.1 27.8 %copy-start.62 = (pred[8,8,128]{2,1,0:T(8,128)(4,1)}, pred[8,8,128]{2,1,0:T(8,128)(4,1)S(1)}, u32[]{:S(2)}) copy-start(pred[8,8,128]{2,1,0:T(8,128)(4,1)S(1)} %get-tuple-element.197) | copy-start | bytes 24580
  11.1 27.8 %copy-start.68 = (pred[8,8,128]{2,1,0:T(8,128)(4,1)}, pred[8,8,128]{2,1,0:T(8,128)(4,1)S(1)}, u32[]{:S(2)}) copy-start(pred[8,8,128]{2,1,0:T(8,128)(4,1)S(1)} %get-tuple-element.196) | copy-start | bytes 24580
  11.1 27.8 %copy-start.74 = (pred[8,8,128]{2,1,0:T(8,128)(4,1)}, pred[8,8,128]{2,1,0:T(8,128)(4,1)S(1)}, u32[]{:S(2)}) copy-start(pred[8,8,128]{2,1,0:T(8,128)(4,1)S(1)} %get-tuple-element.195) | copy-start | bytes 24580
  11.1 27.8 %copy-start.80 = (pred[8,8,128]{2,1,0:T(8,128)(4,1)}, pred[8,8,128]{2,1,0:T(8,128)(4,1)S(1)}, u32[]{:S(2)}) copy-start(pred[8,8,128]{2,1,0:T(8,128)(4,1)S(1)} %get-tuple-element.194) | copy-start | bytes 24580
  11.1 27.8 %copy-start.86 = (pred[8,8,128]{2,1,0:T(8,128)(4,1)}, pred[8,8,128]{2,1,0:T(8,128)(4,1)S(1)}, u32[]{:S(2)}) copy-start(pred[8,8,128]{2,1,0:T(8,128)(4,1)S(1)} %get-tuple-element.193) | copy-start | bytes 24580
  11.1 29.3 %copy-start.28 = (pred[8,8,128]{2,1,0:T(8,128)(4,1)}, pred[8,8,128]{2,1,0:T(8,128)(4,1)S(1)}, u32[]{:S(2)}) copy-start(pred[8,8,128]{2,1,0:T(8,128)(4,1)S(1)} %get-tuple-element.192) | copy-start | bytes 24580
  11.1 29.3 %copy-start.36 = (pred[8,8,128]{2,1,0:T(8,128)(4,1)}, pred[8,8,128]{2,1,0:T(8,128)(4,1)S(1)}, u32[]{:S(2)}) copy-start(pred[8,8,128]{2,1,0:T(8,128)(4,1)S(1)} %get-tuple-element.191) | copy-start | bytes 24580
  11.1 29.3 %copy-start.44 = (pred[8,8,128]{2,1,0:T(8,128)(4,1)}, pred[8,8,128]{2,1,0:T(8,128)(4,1)S(1)}, u32[]{:S(2)}) copy-start(pred[8,8,128]{2,1,0:T(8,128)(4,1)S(1)} %get-tuple-element.190) | copy-start | bytes 24580
  11.1 29.3 %copy-start.60 = (pred[8,8,128]{2,1,0:T(8,128)(4,1)}, pred[8,8,128]{2,1,0:T(8,128)(4,1)S(1)}, u32[]{:S(2)}) copy-start(pred[8,8,128]{2,1,0:T(8,128)(4,1)S(1)} %get-tuple-element.189) | copy-start | bytes 24580
  11.2 29.3 %copy-start.96 = (pred[8,8,128]{2,1,0:T(8,128)(4,1)}, pred[8,8,128]{2,1,0:T(8,128)(4,1)S(1)}, u32[]{:S(2)}) copy-start(pred[8,8,128]{2,1,0:T(8,128)(4,1)S(1)} %get-tuple-element.202) | copy-start | bytes 24580
  12.7 29.9 %copy-start.66 = (pred[8,8,128]{2,1,0:T(8,128)(4,1)}, pred[8,8,128]{2,1,0:T(8,128)(4,1)S(1)}, u32[]{:S(2)}) copy-start(pred[8,8,128]{2,1,0:T(8,128)(4,1)S(1)} %get-tuple-element.183) | copy-start | bytes 24580
  12.7 29.9 %copy-start.72 = (pred[8,8,128]{2,1,0:T(8,128)(4,1)}, pred[8,8,128]{2,1,0:T(8,128)(4,1)S(1)}, u32[]{:S(2)}) copy-start(pred[8,8,128]{2,1,0:T(8,128)(4,1)S(1)} %get-tuple-element.182) | copy-start | bytes 24580
  12.7 29.9 %copy-start.78 = (pred[8,8,128]{2,1,0:T(8,128)(4,1)}, pred[8,8,128]{2,1,0:T(8,128)(4,1)S(1)}, u32[]{:S(2)}) copy-start(pred[8,8,128]{2,1,0:T(8,128)(4,1)S(1)} %get-tuple-element.181) | copy-start | bytes 24580
  12.7 29.9 %copy-start.84 = (pred[8,8,128]{2,1,0:T(8,128)(4,1)}, pred[8,8,128]{2,1,0:T(8,128)(4,1)S(1)}, u32[]{:S(2)}) copy-start(pred[8,8,128]{2,1,0:T(8,128)(4,1)S(1)} %get-tuple-element.180) | copy-start | bytes 24580
  12.7 29.9 %copy-start.90 = (pred[8,8,128]{2,1,0:T(8,128)(4,1)}, pred[8,8,128]{2,1,0:T(8,128)(4,1)S(1)}, u32[]{:S(2)}) copy-start(pred[8,8,128]{2,1,0:T(8,128)(4,1)S(1)} %get-tuple-element.179) | copy-start | bytes 24580
  12.7 32.0 %copy-start.64 = (pred[8,8,128]{2,1,0:T(8,128)(4,1)}, pred[8,8,128]{2,1,0:T(8,128)(4,1)S(1)}, u32[]{:S(2)}) copy-start(pred[8,8,128]{2,1,0:T(8,128)(4,1)S(1)} %get-tuple-element.175) | copy-start | bytes 24580
  12.7 32.0 %copy-start.70 = (pred[8,8,128]{2,1,0:T(8,128)(4,1)}, pred[8,8,128]{2,1,0:T(8,128)(4,1)S(1)}, u32[]{:S(2)}) copy-start(pred[8,8,128]{2,1,0:T(8,128)(4,1)S(1)} %get-tuple-element.174) | copy-start | bytes 24580
  12.7 32.0 %copy-start.76 = (pred[8,8,128]{2,1,0:T(8,128)(4,1)}, pred[8,8,128]{2,1,0:T(8,128)(4,1)S(1)}, u32[]{:S(2)}) copy-start(pred[8,8,128]{2,1,0:T(8,128)(4,1)S(1)} %get-tuple-element.173) | copy-start | bytes 24580
  12.7 32.0 %copy-start.82 = (pred[8,8,128]{2,1,0:T(8,128)(4,1)}, pred[8,8,128]{2,1,0:T(8,128)(4,1)S(1)}, u32[]{:S(2)}) copy-start(pred[8,8,128]{2,1,0:T(8,128)(4,1)S(1)} %get-tuple-element.172) | copy-start | bytes 24580
  12.7 32.0 %copy-start.88 = (pred[8,8,128]{2,1,0:T(8,128)(4,1)}, pred[8,8,128]{2,1,0:T(8,128)(4,1)S(1)}, u32[]{:S(2)}) copy-start(pred[8,8,128]{2,1,0:T(8,128)(4,1)S(1)} %get-tuple-element.171) | copy-start | bytes 24580
  18.4 4.4 %collective-permute-start.2 = (f32[10,10,1,128]{3,2,1,0:T(1,128)S(1)}, f32[10,10,1,128]{3,2,1,0:T(1,128)S(1)}, u32[]{:S(2)}, u32[]{:S(2)}) collective-permute-start(f32[10,10,1,128]{3,2,1,0:T(1,128)S(1)} %get-tuple-element.143), channel_id=1, source_target_pairs={{2,0},{4,2},{6,4},{3,1},{5,3},{7,5},{10,8},{12,10},{14,12},{11,9},... | collective-permute-start | bytes 153608 | tf_op jit(solution)/shard_map/ppermute | solution.py:37
  19.7 3.9 %collective-permute-start.3 = (f32[10,10,1,128]{3,2,1,0:T(1,128)S(1)}, f32[10,10,1,128]{3,2,1,0:T(1,128)S(1)}, u32[]{:S(2)}, u32[]{:S(2)}) collective-permute-start(f32[10,10,1,128]{3,2,1,0:T(1,128)S(1)} %get-tuple-element.142), channel_id=1, source_target_pairs={{0,2},{2,4},{4,6},{1,3},{3,5},{5,7},{8,10},{10,12},{12,14},{9,11},... | collective-permute-start | bytes 153608 | tf_op jit(solution)/shard_map/ppermute | solution.py:35
  24.7 8.5 %collective-permute-start.4 = (f32[10,10,10,1]{2,3,1,0:T(1,128)S(1)}, f32[10,10,10,1]{2,3,1,0:T(1,128)S(1)}, u32[]{:S(2)}, u32[]{:S(2)}) collective-permute-start(f32[10,10,10,1]{2,3,1,0:T(1,128)S(1)} %copy.361), channel_id=1, source_target_pairs={{1,0},{3,2},{5,4},{7,6},{9,8},{11,10},{13,12},{15,14},{17,16},{19,... | collective-permute-start | bytes 12008 | tf_op jit(solution)/shard_map/ppermute | solution.py:37
  26.7 7.2 %collective-permute-start.5 = (f32[10,10,10,1]{2,3,1,0:T(1,128)S(1)}, f32[10,10,10,1]{2,3,1,0:T(1,128)S(1)}, u32[]{:S(2)}, u32[]{:S(2)}) collective-permute-start(f32[10,10,10,1]{2,3,1,0:T(1,128)S(1)} %copy.362), channel_id=1, source_target_pairs={{0,1},{2,3},{4,5},{6,7},{8,9},{10,11},{12,13},{14,15},{16,17},{18,... | collective-permute-start | bytes 12008 | tf_op jit(solution)/shard_map/ppermute | solution.py:35
  65.1 7.0 %collective-permute-start.6 = (f32[6,1,10,130]{3,2,1,0:T(8,128)S(1)}, f32[6,1,10,130]{3,2,1,0:T(8,128)S(1)}, u32[]{:S(2)}, u32[]{:S(2)}) collective-permute-start(f32[6,1,10,130]{3,2,1,0:T(8,128)S(1)} %get-tuple-element.128), channel_id=1, source_target_pairs={{0,8},{8,16},{16,24},{1,9},{9,17},{17,25},{2,10},{10,18},{18,26},{... | collective-permute-start | bytes 93608 | tf_op jit(solution)/shard_map/ppermute | solution.py:35
  69.0 7.2 %collective-permute-start.7 = (f32[6,1,10,130]{3,2,1,0:T(8,128)S(1)}, f32[6,1,10,130]{3,2,1,0:T(8,128)S(1)}, u32[]{:S(2)}, u32[]{:S(2)}) collective-permute-start(f32[6,1,10,130]{3,2,1,0:T(8,128)S(1)} %get-tuple-element.129), channel_id=1, source_target_pairs={{8,0},{16,8},{24,16},{9,1},{17,9},{25,17},{10,2},{18,10},{26,18},{... | collective-permute-start | bytes 93608 | tf_op jit(solution)/shard_map/ppermute | solution.py:37
  76.3 3.2 %collective-permute-start.8 = (f32[6,12,1,130]{3,2,1,0:T(1,128)S(1)}, f32[6,12,1,130]{3,2,1,0:T(1,128)S(1)}, u32[]{:S(2)}, u32[]{:S(2)}) collective-permute-start(f32[6,12,1,130]{3,2,1,0:T(1,128)S(1)} %get-tuple-element.126), channel_id=1, source_target_pairs={{0,2},{2,4},{4,6},{1,3},{3,5},{5,7},{8,10},{10,12},{12,14},{9,11},... | collective-permute-start | bytes 112328 | tf_op jit(solution)/shard_map/ppermute | solution.py:35
  78.0 6.0 %collective-permute-start.9 = (f32[6,12,1,130]{3,2,1,0:T(1,128)S(1)}, f32[6,12,1,130]{3,2,1,0:T(1,128)S(1)}, u32[]{:S(2)}, u32[]{:S(2)}) collective-permute-start(f32[6,12,1,130]{3,2,1,0:T(1,128)S(1)} %get-tuple-element.127), channel_id=1, source_target_pairs={{2,0},{4,2},{6,4},{3,1},{5,3},{7,5},{10,8},{12,10},{14,12},{11,9},... | collective-permute-start | bytes 112328 | tf_op jit(solution)/shard_map/ppermute | solution.py:37
  87.1 6.6 %collective-permute-start.10 = (f32[6,12,12,1]{2,3,1,0:T(1,128)S(1)}, f32[6,12,12,1]{2,3,1,0:T(1,128)S(1)}, u32[]{:S(2)}, u32[]{:S(2)}) collective-permute-start(f32[6,12,12,1]{2,3,1,0:T(1,128)S(1)} %copy.346), channel_id=1, source_target_pairs={{0,1},{2,3},{4,5},{6,7},{8,9},{10,11},{12,13},{14,15},{16,17},{18,... | collective-permute-start | bytes 10376 | tf_op jit(solution)/shard_map/ppermute | solution.py:35
  92.0 5.9 %collective-permute-start.11 = (f32[6,12,12,1]{2,3,1,0:T(1,128)S(1)}, f32[6,12,12,1]{2,3,1,0:T(1,128)}, u32[]{:S(2)}, u32[]{:S(2)}) collective-permute-start(f32[6,12,12,1]{2,3,1,0:T(1,128)S(1)} %copy.347), channel_id=1, source_target_pairs={{1,0},{3,2},{5,4},{7,6},{9,8},{11,10},{13,12},{15,14},{17,16},{19,... | collective-permute-start | bytes 10376 | tf_op jit(solution)/shard_map/ppermute | solution.py:37
  105.8 5.7 %collective-permute-start.12 = (f32[28,64]{1,0:T(8,128)S(1)}, f32[28,64]{1,0:T(8,128)S(1)}, u32[]{:S(2)}, u32[]{:S(2)}) collective-permute-start(f32[28,64]{1,0:T(8,128)S(1)} %fusion.54), channel_id=1, source_target_pairs={{1,0},{3,2},{5,4},{7,6},{9,8},{11,10},{13,12},{15,14},{17,16},{19,... | collective-permute-start | bytes 21512 | tf_op jit(solution)/shard_map/ppermute | solution.py:47
  (77 other events, 309.7 us)
where the time goes:
time: 114 us; the launch traced here: 112 us
  other arithmetic  42.7 us (37%)
  starting transfers between devices  31.5 us (28%)
  waiting for transfers between devices  18.3 us (16%)
  local copies, waits for them, and re-layouts  16.1 us (14%)
  between operations  2.66 us (2%)
    ppermute x6, starting transfers between devices, padded_2(): lax.ppermute(tail, axis, [(i, (i + 1) % count) for i in range(ends)])  22.2 us
    ppermute x6, waiting for transfers between devices, padded_2(): lax.ppermute(head, axis, [((i + 1) % count, i) for i in range(ends)])  12.3 us
    ppermute x6, starting transfers between devices, padded_2(): lax.ppermute(head, axis, [((i + 1) % count, i) for i in range(ends)])  7.95 us
    add x6, other arithmetic, contact_terms(): partner = partner + jnp.where(picked_here, windows[number][1], 0.0)  6.21 us
    concatenate x5, other arithmetic, padded_2(): jnp.concatenate([lax.ppermute(tail, axis, [(i, (i + 1) % count) for i in...  4.84 us
    broadcast_in_dim x4, other arithmetic, contact_terms(): jnp.where(slot_live[None], jnp.concatenate([pair_force, torque_center], 0...  4.76 us
    reduce_sum x6, other arithmetic, contact_pair(): distance = jnp.sqrt(jnp.sum(separation * separation, 0))  4.63 us
    unnamed x227, local copies, waits for them, and re-layouts  4.58 us
  transfers between devices with their start and end apart: 13, of which 6 were waited for; matrix products, arithmetic and copies ran while one was open for 13% of the time, Pallas kernels for 0%

commit v1 on v0

v1 whole, which is shorter than its diff:
```python
import functools

import jax
import jax.numpy as jnp
from jax import lax
from jax.experimental import pallas as pl
from jax.experimental.pallas import tpu as pltpu
from jax.sharding import PartitionSpec as P

MESH = pl.DeviceIdType.MESH
AXES = ("gx", "gy", "gz")

forward_dirs = [
    (1, 0, 0),
    (0, 1, 0),
    (0, 0, 1),
    (1, 1, 0),
    (1, -1, 0),
    (1, 0, 1),
    (1, 0, -1),
    (0, 1, 1),
    (0, 1, -1),
]
reach = [
    (1, 0, 0),
    (0, 1, 0),
    (0, -1, 0),
    (0, 0, 1),
    (0, 0, -1),
    (1, 1, 0),
    (1, -1, 0),
    (1, 0, 1),
    (1, 0, -1),
    (0, 1, 1),
    (0, 1, -1),
]
stiff_normal = 10.0
damp_normal = 2.0
stiff_shear = 8.0
damp_shear = 1.5
friction = 0.4
shear_floor = 0.05
time_step = 0.05
gravity = 1.0


def negated(delta):
    return tuple(-step for step in delta)


def dot3(first, second):
    return first[0] * second[0] + first[1] * second[1] + first[2] * second[2]


def cross3(first, second):
    return [
        first[1] * second[2] - first[2] * second[1],
        first[2] * second[0] - first[0] * second[2],
        first[0] * second[1] - first[1] * second[0],
    ]


def kernel(
    sizes,
    offset_in, velocity_in, spin_in, radius_in, history_in, contacts_in, leaving_ref,
    offset_out, velocity_out, spin_out, history_out, arrivals_ref,
    fields, spin, history, contacts, moved, springs_out, stay,
    row_lo, row_hi, halo_yp, halo_ym, face, halo_z,
    sum_c, sum_zp, sum_zm, sum_yp, sum_ym, sum_yzp, sum_yzm,
    rows_p, rows_m, cols, back_x, back_yp, back_ym, back_xy, back_z,
    bottom, picked_rows, outbox, inbox,
    load_sem, store_sem, send_sem, recv_sem, return_send, return_recv, down_sem,
):
    nx = radius_in.shape[0]
    ny, nz = radius_in.shape[1:]
    slots = contacts_in.shape[0]
    me = [lax.axis_index(axis) for axis in AXES]
    f32 = jnp.float32

    def there(delta):
        flag = None
        for place, size, step in zip(me, sizes, delta):
            if step:
                one = (place < size - 1) if step > 0 else (place > 0)
                flag = one if flag is None else jnp.logical_and(flag, one)
        return flag

    def device(delta):
        return tuple(place + step for place, step in zip(me, delta))

    loads = []
    for number, (source, target) in enumerate(
        (
            (offset_in, fields.at[0:3, 0:nx]),
            (velocity_in, fields.at[3:6, 0:nx]),
            (spin_in, spin),
            (radius_in, fields.at[9, 0:nx]),
            (contacts_in, contacts),
            (history_in, history),
        )
    ):
        loads.append(pltpu.make_async_copy(source, target, load_sem.at[number]))
        loads[-1].start()

    barrier = pltpu.get_barrier_semaphore()
    greeted = jnp.int32(0)
    neighbours = []
    for delta in reach:
        for way in (delta, negated(delta)):
            if way not in neighbours:
                neighbours.append(way)
    for way in neighbours:
        flag = there(way)
        greeted = greeted + flag.astype(jnp.int32)

        @pl.when(flag)
        def _(way=way):
            pl.semaphore_signal(barrier, inc=1, device_id=device(way), device_id_type=MESH)

    tile = (ny, nz)
    lane = lax.broadcasted_iota(jnp.int32, tile, 1)
    sub = lax.broadcasted_iota(jnp.int32, tile, 0)
    zero = jnp.zeros(tile, f32)

    def col(value, at):
        return jnp.broadcast_to(value[:, at : at + 1], tile)

    def row(ref, *at):
        return jnp.broadcast_to(ref[at[0], at[1] : at[1] + 1, :], tile)

    def turn_z(value, by):
        return pltpu.roll(value, by % nz, 1)

    def turn_y(value, by):
        return pltpu.roll(value, by % ny, 0)

    leaving = leaving_ref[0, 0]
    wide = jnp.broadcast_to(leaving, (ny, leaving.shape[1]))
    wide_sub = lax.broadcasted_iota(jnp.int32, wide.shape, 0)

    def mark(x, carry):
        gone = zero
        for z in range(2):
            hit = (wide == (x * ny + wide_sub) * nz + z).astype(f32)
            gone = gone + jnp.where(lane == z, jnp.sum(hit, 1, keepdims=True), 0.0)
        stay[x] = 1.0 - gone
        return carry

    lax.fori_loop(0, nx, mark, 0)

    halo_at = [
        fields.at[:, nx],
        halo_yp.at[0:nx],
        halo_ym.at[0:nx],
        halo_z.at[0],
        halo_z.at[1],
        halo_yp.at[nx],
        halo_ym.at[nx],
        halo_z.at[2],
        halo_z.at[3],
        halo_z.at[4],
        halo_z.at[5],
    ]
    back_at = [
        back_x,
        back_yp,
        back_ym,
        back_z.at[0],
        back_z.at[1],
        back_xy.at[0],
        back_xy.at[1],
        back_z.at[2],
        back_z.at[3],
        back_z.at[4],
        back_z.at[5],
    ]
    for delta, halo, back in zip(reach, halo_at, back_at):

        @pl.when(jnp.logical_not(there(delta)))
        def _(halo=halo):
            halo[...] = jnp.zeros(halo.shape, f32)

        @pl.when(jnp.logical_not(there(negated(delta))))
        def _(back=back):
            back[...] = jnp.zeros(back.shape, f32)

    for number in range(6):
        for part in (sum_c, sum_zp, sum_zm, sum_yp, sum_ym):
            part[number, 0] = zero
        for part in (sum_yzp, sum_yzm):
            part[number, nx] = zero

    for number in range(4):
        loads[number].wait()

    def pack(x, faces):
        low, high = faces
        for k in range(3):
            fields[6 + k, x] = spin[k, x] * fields[9, x]
        for c in range(10):
            value = fields[c, x]
            row_lo[x, c : c + 1, :] = value[0:1]
            row_hi[x, c : c + 1, :] = value[ny - 1 : ny]
            here = lane == x * 10 + c
            low = jnp.where(here, col(value, 0), low)
            high = jnp.where(here, col(value, nz - 1), high)
        return low, high

    low, high = lax.fori_loop(0, nx, pack, (zero, zero))
    face[0] = low
    face[1] = high

    pl.semaphore_wait(barrier, greeted)

    sent_from = [
        fields.at[:, 0],
        row_lo,
        row_hi,
        face.at[0],
        face.at[1],
        row_lo.at[0],
        row_hi.at[0],
        face.at[0],
        face.at[1],
        face.at[0],
        face.at[1],
    ]
    order = [5, 6, 7, 8, 9, 10, 0, 1, 2, 3, 4]
    sends = []
    for number, delta in enumerate(reach):
        sends.append(
            pltpu.make_async_remote_copy(
                src_ref=sent_from[number],
                dst_ref=halo_at[number],
                send_sem=send_sem.at[number],
                recv_sem=recv_sem.at[number],
                device_id=device(negated(delta)),
                device_id_type=MESH,
            )
        )
    for number in order:

        @pl.when(there(negated(reach[number])))
        def _(number=number):
            sends[number].start()

    loads[4].wait()
    loads[5].wait()
    for number in range(len(reach)):

        @pl.when(there(reach[number]))
        def _(number=number):
            sends[number].wait_recv()

    span = nx * 10
    col_zp = jnp.where(lane < span, halo_z[0], turn_z(halo_z[2], span))
    col_zm = jnp.where(lane < span, halo_z[1], turn_z(halo_z[3], span))
    col_yzp = jnp.where(sub == ny - 1, turn_y(halo_z[4], -1), turn_y(col_zp, -1))
    col_yzm = jnp.where(sub == ny - 1, turn_y(halo_z[5], -1), turn_y(col_zm, -1))

    def pairs(x, carry):
        own = [fields[c, x] for c in range(10)]
        codes = [contacts[s, x] for s in range(slots)]
        own_sum = [zero] * 6
        springs = []
        for number, (dx, dy, dz) in enumerate(forward_dirs):
            at = x + dx
            other = []
            if dz:
                source = {(0, 1): col_zp, (0, -1): col_zm, (1, 1): col_yzp, (1, -1): col_yzm}[(dy, dz)]
                rim = pltpu.roll(source, nz - at * 10, 1)
            for c in range(10):
                value = fields[c, at]
                if dy > 0:
                    value = jnp.where(sub == ny - 1, row(halo_yp, at, c), turn_y(value, -1))
                elif dy < 0:
                    value = jnp.where(sub == 0, row(halo_ym, at, c), turn_y(value, 1))
                if dz > 0:
                    value = jnp.where(lane == nz - 1, turn_z(rim, nz - 1 - c), turn_z(value, -1))
                elif dz < 0:
                    value = jnp.where(lane == 0, turn_z(rim, -c), turn_z(value, 1))
                other.append(value)
            shear = [zero] * 3
            live = None
            for s in range(slots):
                hit = codes[s] == number
                live = hit if live is None else jnp.logical_or(live, hit)
                for k in range(3):
                    shear[k] = jnp.where(hit, history[s, k, x], shear[k])
            apart = [other[k] - own[k] for k in range(3)]
            for k, step in enumerate((dx, dy, dz)):
                if step:
                    apart[k] = (float(step) + other[k]) - own[k]
            square = dot3(apart, apart)
            inverse = lax.rsqrt(square)
            normal = [part * inverse for part in apart]
            radius_sum = own[9] + other[9]
            inter = jnp.maximum(radius_sum - square * inverse, 0.0)
            contact = jnp.sqrt(own[9] * other[9] / radius_sum * inter)
            turned = cross3([own[6 + k] + other[6 + k] for k in range(3)], normal)
            relative = [other[3 + k] - own[3 + k] - turned[k] for k in range(3)]
            approach = dot3(relative, normal)
            sliding = [relative[k] - approach * normal[k] for k in range(3)]
            repulsion = jnp.maximum(contact * (stiff_normal * inter - damp_normal * approach), 0.0)
            along = dot3(shear, normal)
            spring = [shear[k] - along * normal[k] + time_step * sliding[k] for k in range(3)]
            trial = [contact * (stiff_shear * spring[k] + damp_shear * sliding[k]) for k in range(3)]
            scale = lax.rsqrt(jnp.maximum(dot3(trial, trial), shear_floor * shear_floor))
            factor = jnp.minimum(1.0, friction * repulsion * scale)
            factor = jnp.where(live, factor, 0.0)
            repulsion = jnp.where(live, repulsion, 0.0)
            tangent = [factor * trial[k] for k in range(3)]
            pair = [tangent[k] - repulsion * normal[k] for k in range(3)]
            terms = pair + cross3(normal, tangent)
            springs.append([factor * spring[k] for k in range(3)])
            for c in range(6):
                own_sum[c] = own_sum[c] + terms[c]
            react = [-terms[c] if c < 3 else terms[c] for c in range(6)]
            into = {
                (0, 0): sum_c, (0, 1): sum_zp, (0, -1): sum_zm,
                (1, 0): sum_yp, (-1, 0): sum_ym, (1, 1): sum_yzp, (1, -1): sum_yzm,
            }[(dy, dz)]
            for c in range(6):
                if dx or (dy and dz):
                    into[c, at] = react[c]
                else:
                    into[c, at] += react[c]
        for c in range(6):
            sum_c[c, x] += own_sum[c]
        staying = stay[x]
        packed = jnp.where(lane // 2 == 9, turn_z(own[9], 18), 0.0)
        for s in range(slots):
            for k in range(3):
                value = zero
                for number in range(len(forward_dirs)):
                    value = jnp.where(codes[s] == number, springs[number][k], value)
                springs_out[s, k, x] = value * staying
                place = 10 + 3 * s + k
                packed = jnp.where(lane // 2 == place, turn_z(value, 2 * place), packed)
        bottom[x] = packed
        return carry

    lax.fori_loop(0, nx, pairs, 0)

    history_store = pltpu.make_async_copy(springs_out, history_out, store_sem.at[0])
    history_store.start()

    def split(x, carry):
        face_p, face_m, edge_p, edge_m = carry
        for c in range(6):
            zp, zm = sum_zp[c, x], sum_zm[c, x]
            yp, ym = sum_yp[c, x], sum_ym[c, x]
            yzp, yzm = sum_yzp[c, x], sum_yzm[c, x]
            up = yp + jnp.where(lane == 0, 0.0, turn_z(yzp, 1))
            up = up + jnp.where(lane == nz - 1, 0.0, turn_z(yzm, -1))
            total = sum_c[c, x] + jnp.where(lane == 0, 0.0, turn_z(zp, 1))
            total = total + jnp.where(lane == nz - 1, 0.0, turn_z(zm, -1))
            total = total + jnp.where(sub == 0, 0.0, turn_y(up, 1))
            total = total + jnp.where(sub == ny - 1, 0.0, turn_y(ym, -1))
            sum_c[c, x] = total
            rows_p[x, c : c + 1, :] = up[ny - 1 : ny]
            rows_m[x, c : c + 1, :] = ym[0:1]
            corner_p, corner_m = turn_y(yzp, 1), turn_y(yzm, 1)
            here = lane == x * 8 + c
            face_p = jnp.where(here, col(zp + jnp.where(sub == 0, 0.0, corner_p), nz - 1), face_p)
            face_m = jnp.where(here, col(zm + jnp.where(sub == 0, 0.0, corner_m), 0), face_m)
            edge_p = jnp.where(here, col(corner_p, nz - 1), edge_p)
            edge_m = jnp.where(here, col(corner_m, 0), edge_m)
        return face_p, face_m, edge_p, edge_m

    tiles = lax.fori_loop(0, nx + 1, split, (zero,) * 4)
    for number in range(4):
        cols[number] = tiles[number]

    returned_from = [
        sum_c.at[:, nx],
        rows_p.at[0:nx],
        rows_m.at[0:nx],
        cols.at[0],
        cols.at[1],
        rows_p.at[nx],
        rows_m.at[nx],
        cols.at[0],
        cols.at[1],
        cols.at[2],
        cols.at[3],
    ]
    returns = []
    for number, delta in enumerate(reach):
        returns.append(
            pltpu.make_async_remote_copy(
                src_ref=returned_from[number],
                dst_ref=back_at[number],
                send_sem=return_send.at[number],
                recv_sem=return_recv.at[number],
                device_id=device(delta),
                device_id_type=MESH,
            )
        )
    for number in order:

        @pl.when(there(reach[number]))
        def _(number=number):
            returns[number].start()

    for number, delta in enumerate(reach):

        @pl.when(there(negated(delta)))
        def _(number=number):
            returns[number].wait_recv()

    for c in range(6):
        sum_c[c, 0] += back_x[c]
    back_yp[0] += back_xy[0]
    back_ym[0] += back_xy[1]
    in_zp = back_z[0] + jnp.where(lane < 8, turn_z(back_z[2], -8 * nx), 0.0)
    in_zm = back_z[1] + jnp.where(lane < 8, turn_z(back_z[3], -8 * nx), 0.0)
    in_zp = in_zp + jnp.where(sub == 0, back_z[4], 0.0)
    in_zm = in_zm + jnp.where(sub == 0, back_z[5], 0.0)

    def finish(x, carry):
        staying = stay[x]
        radius = fields[9, x]
        inverse = 1.0 / radius
        cubed = inverse * inverse * inverse
        from_zp = pltpu.roll(in_zp, nz - 8 * x, 1)
        from_zm = pltpu.roll(in_zm, nz - 8 * x, 1)
        totals = []
        for c in range(6):
            total = sum_c[c, x]
            total = total + jnp.where(sub == 0, row(back_yp, x, c), 0.0)
            total = total + jnp.where(sub == ny - 1, row(back_ym, x, c), 0.0)
            total = total + jnp.where(lane == 0, turn_z(from_zp, -c), 0.0)
            total = total + jnp.where(lane == nz - 1, turn_z(from_zm, nz - 1 - c), 0.0)
            totals.append(total)
        coords = (
            (me[0] * nx + x).astype(f32),
            (me[1] * ny + sub).astype(f32),
            (me[2] * nz + lane).astype(f32),
        )
        twisted = (time_step / 0.4) * cubed * inverse
        packed = bottom[x]
        for k in range(3):
            push = totals[k] * cubed
            if k == 2:
                push = push - gravity
            new_velocity = fields[3 + k, x] + time_step * push
            new_spin = spin[k, x] + twisted * totals[3 + k]
            new_offset = fields[k, x] + time_step * new_velocity
            moved[k, x] = new_offset * staying
            moved[3 + k, x] = new_velocity * staying
            moved[6 + k, x] = new_spin * staying
            for place, value in ((k, coords[k] + new_offset), (3 + k, new_velocity), (6 + k, new_spin)):
                packed = jnp.where(lane // 2 == place, turn_z(value, 2 * place), packed)
        bottom[x] = packed
        return carry

    lax.fori_loop(0, nx, finish, 0)

    stores = [history_store]
    for number, target in enumerate((offset_out, velocity_out, spin_out)):
        stores.append(
            pltpu.make_async_copy(moved.at[3 * number : 3 * number + 3], target, store_sem.at[1 + number])
        )
        stores[-1].start()

    cells = bottom[...].reshape(nx * ny, nz)
    capacity = leaving.shape[1]
    cell_number = lax.broadcasted_iota(jnp.int32, (nx * ny, capacity), 0) * nz
    chosen = []
    for z in range(2):
        selector = (cell_number + z == leaving).astype(f32)
        chosen.append(
            lax.dot_general(
                cells, selector, (((0,), (0,)), ((), ())),
                precision=lax.Precision.HIGHEST, preferred_element_type=f32,
            )
        )
    parity = lax.broadcasted_iota(jnp.int32, chosen[0].shape, 0) % 2
    picked_rows[:, 0:capacity] = jnp.where(parity == 0, chosen[0], chosen[1])
    rows = outbox.shape[0]
    outbox[...] = picked_rows[pl.ds(0, rows, stride=2), :] + picked_rows[pl.ds(1, rows, stride=2), :]
    down = pltpu.make_async_remote_copy(
        src_ref=outbox,
        dst_ref=inbox,
        send_sem=down_sem.at[0],
        recv_sem=down_sem.at[1],
        device_id=device((0, 0, -1)),
        device_id_type=MESH,
    )
    has_below, has_above = there((0, 0, -1)), there((0, 0, 1))

    @pl.when(has_below)
    def _():
        down.start()

    for number, delta in enumerate(reach):

        @pl.when(there(negated(delta)))
        def _(number=number):
            sends[number].wait_send()

        @pl.when(there(delta))
        def _(number=number):
            returns[number].wait_send()

    for store in stores:
        store.wait()

    @pl.when(has_below)
    def _():
        down.wait_send()

    @pl.when(has_above)
    def _():
        down.wait_recv()
        arrivals_ref[...] = inbox[:, 0:capacity]

    @pl.when(jnp.logical_not(has_above))
    def _():
        arrivals_ref[...] = jnp.zeros(arrivals_ref.shape, f32)


def on_device(sizes, offset, velocity, spin, radius, history, contacts, leaving):
    nx, ny, nz = radius.shape
    slots = contacts.shape[0]
    rows = 10 + 3 * slots
    capacity = leaving.shape[-1]
    f32 = jnp.float32
    anywhere = pl.BlockSpec(memory_space=pl.ANY)
    near = pl.BlockSpec(memory_space=pltpu.VMEM)
    count = len(reach)
    vmem = lambda *shape: pltpu.VMEM(shape, f32)
    dma = lambda size: pltpu.SemaphoreType.DMA((size,))
    outs = pl.pallas_call(
        functools.partial(kernel, sizes),
        out_shape=(
            jax.ShapeDtypeStruct(offset.shape, f32),
            jax.ShapeDtypeStruct(velocity.shape, f32),
            jax.ShapeDtypeStruct(spin.shape, f32),
            jax.ShapeDtypeStruct(history.shape, f32),
            jax.ShapeDtypeStruct((rows, capacity), f32),
        ),
        in_specs=[anywhere] * 6 + [near],
        out_specs=(anywhere,) * 4 + (near,),
        scratch_shapes=[
            vmem(10, nx + 1, ny, nz),
            vmem(3, nx, ny, nz),
            vmem(slots, 3, nx, ny, nz),
            pltpu.VMEM((slots, nx, ny, nz), jnp.int32),
            vmem(9, nx, ny, nz),
            vmem(slots, 3, nx, ny, nz),
            vmem(nx, ny, nz),
            vmem(nx, 16, nz),
            vmem(nx, 16, nz),
            vmem(nx + 1, 16, nz),
            vmem(nx + 1, 16, nz),
            vmem(2, ny, nz),
            vmem(6, ny, nz),
            *[vmem(6, nx + 1, ny, nz) for part in range(7)],
            vmem(nx + 1, 8, nz),
            vmem(nx + 1, 8, nz),
            vmem(4, ny, nz),
            vmem(6, ny, nz),
            vmem(nx, 8, nz),
            vmem(nx, 8, nz),
            vmem(2, 8, nz),
            vmem(6, ny, nz),
            vmem(nx, ny, nz),
            vmem(nz, nz),
            vmem(rows, nz),
            vmem(rows, nz),
            dma(6),
            dma(4),
            dma(count),
            dma(count),
            dma(count),
            dma(count),
            dma(2),
        ],
        compiler_params=pltpu.CompilerParams(collective_id=0, has_side_effects=True),
    )(offset, velocity, spin, radius, history, contacts, leaving)
    return (*outs[:4], outs[4].reshape(rows, 1, 1, 1, capacity))


def solution(mesh):
    cells = P(None, "gx", "gy", "gz")
    sizes = tuple(mesh.shape[axis] for axis in AXES)
    return jax.shard_map(
        functools.partial(on_device, sizes),
        mesh=mesh,
        in_specs=(
            cells,
            cells,
            cells,
            P("gx", "gy", "gz"),
            P(None, None, "gx", "gy", "gz"),
            cells,
            P("gx", "gy", "gz", None),
        ),
        out_specs=(cells, cells, cells, P(None, None, "gx", "gy", "gz"), P(None, "gx", "gy", "gz", None)),
        check_vma=False,
    )
```

time: 114 us -> 29.7 us (0.26); the launches traced: 112 us -> 29.4 us
  other arithmetic: 42.7 us -> 0 us
  starting transfers between devices: 31.5 us -> 0 us
  Pallas kernels: 0 us -> 21.9 us
  waiting for transfers between devices: 18.3 us -> 0 us
  local copies, waits for them, and re-layouts: 16.1 us -> 6.83 us
  between operations: 2.66 us -> 0.65 us
    ppermute x13 -> x0, starting transfers between devices: 31.5 us -> none  [the longest x6 22.2 us: padded_2(): lax.ppermute(tail, axis, [(i, (i + 1) % count) for i in range(ends)])]
    pallas_call x0 -> x1, Pallas kernels: none -> 21.9 us  [on_device(): pl.pallas_call(functools.partial(kernel, sizes), out_shape=(jax.ShapeDtyp...]
    ppermute x13 -> x0, waiting for transfers between devices: 18.3 us -> none  [the longest x6 12.3 us: padded_2(): lax.ppermute(head, axis, [((i + 1) % count, i) for i in range(ends)])]
    add x24 -> x0, other arithmetic: 14.1 us -> none  [the longest x6 6.21 us: contact_terms(): partner = partner + jnp.where(picked_here, windows[number][1], 0.0)]
    concatenate x8 -> x0, other arithmetic: 6.07 us -> none  [the longest x5 4.84 us: padded_2(): jnp.concatenate([lax.ppermute(tail, axis, [(i, (i + 1) % count) for i in...]
    reduce_sum x11 -> x0, other arithmetic: 5.97 us -> none  [the longest x6 4.63 us: contact_pair(): distance = jnp.sqrt(jnp.sum(separation * separation, 0))]
    mul x14 -> x0, other arithmetic: 5.3 us -> none  [the longest x3 2.15 us: contact_pair(): radius_partner * twisting]
    slice x10 -> x0, local copies, waits for them, and re-layouts: 5.19 us -> none  [the longest x3 2.79 us: padded_2(): lax.slice_in_dim(cells, cells.shape[dim] - width, cells.shape[dim], axis=...]
  transfers between devices with their start and end apart: 13 -> 0, of which waited for: 6 -> 0; matrix products, arithmetic and copies ran while one was open for 13% -> 0% of each run, Pallas kernels for 0% -> 0%
where the time goes in v1:
time: 29.7 us; the launch traced here: 29.4 us
  Pallas kernels  21.9 us (74%)
  local copies, waits for them, and re-layouts  6.83 us (23%)
  between operations  0.65 us (2%)
    pallas_call x1, Pallas kernels, on_device(): pl.pallas_call(functools.partial(kernel, sizes), out_shape=(jax.ShapeDtyp...  21.9 us
    unnamed x7, local copies, waits for them, and re-layouts  6.83 us

profile of v1, /device:TPU:0, one launch (start us, length us, event | category | flops | bytes accessed | tf_op | source)
XLA Modules:
  0.0 29.4 jit_solution(14835225758970428644)
XLA Ops:
  0.6 21.9 %shard_map.110 = (f32[3,8,8,128]{3,2,1,0:T(8,128)}, f32[3,8,8,128]{3,2,1,0:T(8,128)}, f32[3,8,8,128]{3,2,1,0:T(8,128)}, f32[6,3,8,8,128]{4,3,2,1,0:T(8,128)}, f32[28,64]{1,0:T(8,128)}) custom-call(f32[3,8,8,128]{3,2,1,0:T(8,128)} %offset_in.1, f32[3,8,8,128]{3,2,1,0:T(8,128)} %velocity_in.1, f32[3,8,8,128]{3,2,1,0:T(8,128)} %spin_in.1, ...), custom_call_target="tpu_custom_call" | custom-call | tf_op jit(solution)/shard_map/pallas_call | solution.py:535
  22.6 0.0 copy-start
  22.6 1.4 %copy.12 = f32[28,1,1,1,64]{4,3,2,1,0:T(1,128)} copy(f32[28,1,1,1,64]{4,0,3,2,1:T(8,128)} %bitcast.1) | data formatting | bytes 14336
  24.0 1.5 %copy.17 = f32[3,8,8,128]{3,2,1,0:T(8,128)} copy(f32[3,8,8,128]{3,2,1,0:T(8,128)} %get-tuple-element.25) | data formatting | bytes 196608
  25.5 1.5 %copy.18 = f32[3,8,8,128]{3,2,1,0:T(8,128)} copy(f32[3,8,8,128]{3,2,1,0:T(8,128)} %get-tuple-element.26) | data formatting | bytes 196608
  27.1 1.5 %copy.19 = f32[3,8,8,128]{3,2,1,0:T(8,128)} copy(f32[3,8,8,128]{3,2,1,0:T(8,128)} %get-tuple-element.27) | data formatting | bytes 196608
  28.6 0.0 copy-done
  28.6 0.8 %copy.20 = f32[6,3,8,8,128]{4,3,2,1,0:T(8,128)} copy(f32[6,3,8,8,128]{4,3,2,1,0:T(8,128)S(1)} %copy-done) | data formatting | bytes 1179648
Async XLA Ops:
  22.6 6.0 %copy-start = (f32[6,3,8,8,128]{4,3,2,1,0:T(8,128)S(1)}, f32[6,3,8,8,128]{4,3,2,1,0:T(8,128)}, u32[]{:S(2)}) copy-start(f32[6,3,8,8,128]{4,3,2,1,0:T(8,128)} %get-tuple-element.28) | copy-start | bytes 1769476

commit v2 on v1

--- a/solution.py
+++ b/solution.py
@@ -60,16 +60,30 @@
     ]
 
 
+def loop(count, body, carry, unroll):
+    if unroll >= count:
+        for at in range(count):
+            carry = body(at, carry)
+        return carry
+
+    def some(step, carry):
+        for part in range(unroll):
+            carry = body(step * unroll + part, carry)
+        return carry
+
+    return lax.fori_loop(0, count // unroll, some, carry)
+
+
 def kernel(
     sizes,
     offset_in, velocity_in, spin_in, radius_in, history_in, contacts_in, leaving_ref,
-    offset_out, velocity_out, spin_out, history_out, arrivals_ref,
-    fields, spin, history, contacts, moved, springs_out, stay,
+    moved, springs_out, arrivals_ref,
+    fields, spin, history, contacts, stay,
     row_lo, row_hi, halo_yp, halo_ym, face, halo_z,
     sum_c, sum_zp, sum_zm, sum_yp, sum_ym, sum_yzp, sum_yzm,
     rows_p, rows_m, cols, back_x, back_yp, back_ym, back_xy, back_z,
     bottom, picked_rows, outbox, inbox,
-    load_sem, store_sem, send_sem, recv_sem, return_send, return_recv, down_sem,
+    load_sem, send_sem, recv_sem, return_send, return_recv, down_sem,
 ):
     nx = radius_in.shape[0]
     ny, nz = radius_in.shape[1:]
@@ -131,6 +145,9 @@
     def turn_z(value, by):
         return pltpu.roll(value, by % nz, 1)
 
+    def turn_x(value, back):
+        return pltpu.roll(value, (nz - back) % nz if isinstance(back, int) else nz - back, 1)
+
     def turn_y(value, by):
         return pltpu.roll(value, by % ny, 0)
 
@@ -146,7 +163,7 @@
         stay[x] = 1.0 - gone
         return carry
 
-    lax.fori_loop(0, nx, mark, 0)
+    loop(nx, mark, 0, nx)
 
     halo_at = [
         fields.at[:, nx],
@@ -206,7 +223,7 @@
             high = jnp.where(here, col(value, nz - 1), high)
         return low, high
 
-    low, high = lax.fori_loop(0, nx, pack, (zero, zero))
+    low, high = loop(nx, pack, (zero, zero), nx)
     face[0] = low
     face[1] = high
 
@@ -268,7 +285,7 @@
             other = []
             if dz:
                 source = {(0, 1): col_zp, (0, -1): col_zm, (1, 1): col_yzp, (1, -1): col_yzm}[(dy, dz)]
-                rim = pltpu.roll(source, nz - at * 10, 1)
+                rim = turn_x(source, at * 10)
             for c in range(10):
                 value = fields[c, at]
                 if dy > 0:
@@ -340,10 +357,7 @@
         bottom[x] = packed
         return carry
 
-    lax.fori_loop(0, nx, pairs, 0)
-
-    history_store = pltpu.make_async_copy(springs_out, history_out, store_sem.at[0])
-    history_store.start()
+    loop(nx, pairs, 0, 1)
 
     def split(x, carry):
         face_p, face_m, edge_p, edge_m = carry
@@ -368,7 +382,7 @@
             edge_m = jnp.where(here, col(corner_m, 0), edge_m)
         return face_p, face_m, edge_p, edge_m
 
-    tiles = lax.fori_loop(0, nx + 1, split, (zero,) * 4)
+    tiles = loop(nx + 1, split, (zero,) * 4, nx + 1)
     for number in range(4):
         cols[number] = tiles[number]
 
@@ -423,8 +437,8 @@
         radius = fields[9, x]
         inverse = 1.0 / radius
         cubed = inverse * inverse * inverse
-        from_zp = pltpu.roll(in_zp, nz - 8 * x, 1)
-        from_zm = pltpu.roll(in_zm, nz - 8 * x, 1)
+        from_zp = turn_x(in_zp, 8 * x)
+        from_zm = turn_x(in_zm, 8 * x)
         totals = []
         for c in range(6):
             total = sum_c[c, x]
@@ -455,14 +469,7 @@
         bottom[x] = packed
         return carry
 
-    lax.fori_loop(0, nx, finish, 0)
-
-    stores = [history_store]
-    for number, target in enumerate((offset_out, velocity_out, spin_out)):
-        stores.append(
-            pltpu.make_async_copy(moved.at[3 * number : 3 * number + 3], target, store_sem.at[1 + number])
-        )
-        stores[-1].start()
+    loop(nx, finish, 0, nx)
 
     cells = bottom[...].reshape(nx * ny, nz)
     capacity = leaving.shape[1]
@@ -504,9 +511,6 @@
         def _(number=number):
             returns[number].wait_send()
 
-    for store in stores:
-        store.wait()
-
     @pl.when(has_below)
     def _():
         down.wait_send()
@@ -519,6 +523,19 @@
     @pl.when(jnp.logical_not(has_above))
     def _():
         arrivals_ref[...] = jnp.zeros(arrivals_ref.shape, f32)
+
+
+def emit(moved, springs, arrived, offset_out, velocity_out, spin_out, history_out, arrivals, sem):
+    copies = [pltpu.make_async_copy(springs, history_out, sem.at[3])]
+    for number, target in enumerate((offset_out, velocity_out, spin_out)):
+        source = moved.at[3 * number : 3 * number + 3]
+        copies.append(pltpu.make_async_copy(source, target, sem.at[number]))
+    for copy in copies:
+        copy.start()
+    for place in range(arrived.shape[0]):
+        arrivals[place, 0, 0] = arrived[place : place + 1, :]
+    for copy in copies:
+        copy.wait()
 
 
 def on_device(sizes, offset, velocity, spin, radius, history, contacts, leaving):
@@ -532,24 +549,20 @@
     count = len(reach)
     vmem = lambda *shape: pltpu.VMEM(shape, f32)
     dma = lambda size: pltpu.SemaphoreType.DMA((size,))
-    outs = pl.pallas_call(
+    moved, springs, arrived = pl.pallas_call(
         functools.partial(kernel, sizes),
         out_shape=(
-            jax.ShapeDtypeStruct(offset.shape, f32),
-            jax.ShapeDtypeStruct(velocity.shape, f32),
-            jax.ShapeDtypeStruct(spin.shape, f32),
-            jax.ShapeDtypeStruct(history.shape, f32),
-            jax.ShapeDtypeStruct((rows, capacity), f32),
+            pltpu.VMEM((9, nx, ny, nz), f32),
+            pltpu.VMEM(history.shape, f32),
+            pltpu.VMEM((rows, capacity), f32),
         ),
         in_specs=[anywhere] * 6 + [near],
-        out_specs=(anywhere,) * 4 + (near,),
+        out_specs=(near,) * 3,
         scratch_shapes=[
             vmem(10, nx + 1, ny, nz),
             vmem(3, nx, ny, nz),
             vmem(slots, 3, nx, ny, nz),
             pltpu.VMEM((slots, nx, ny, nz), jnp.int32),
-            vmem(9, nx, ny, nz),
-            vmem(slots, 3, nx, ny, nz),
             vmem(nx, ny, nz),
             vmem(nx, 16, nz),
             vmem(nx, 16, nz),
@@ -571,7 +584,6 @@
             vmem(rows, nz),
             vmem(rows, nz),
             dma(6),
-            dma(4),
             dma(count),
             dma(count),
             dma(count),
@@ -580,7 +592,19 @@
         ],
         compiler_params=pltpu.CompilerParams(collective_id=0, has_side_effects=True),
     )(offset, velocity, spin, radius, history, contacts, leaving)
-    return (*outs[:4], outs[4].reshape(rows, 1, 1, 1, capacity))
+    return pl.pallas_call(
+        emit,
+        out_shape=(
+            jax.ShapeDtypeStruct(offset.shape, f32),
+            jax.ShapeDtypeStruct(velocity.shape, f32),
+            jax.ShapeDtypeStruct(spin.shape, f32),
+            jax.ShapeDtypeStruct(history.shape, f32),
+            jax.ShapeDtypeStruct((rows, 1, 1, 1, capacity), f32),
+        ),
+        in_specs=[near] * 3,
+        out_specs=(anywhere,) * 4 + (near,),
+        scratch_shapes=[dma(4)],
+    )(*[pltpu.with_memory_space_constraint(part, pltpu.MemorySpace.VMEM) for part in (moved, springs, arrived)])
 
 
 def solution(mesh):

time: 29.7 us -> 21.7 us (0.73)
  local copies, waits for them, and re-layouts: 6.83 us -> 0 us
  Pallas kernels: 21.9 us -> 20.9 us
    unnamed x7 -> x0, local copies, waits for them, and re-layouts: 6.83 us -> none
    pallas_call x1 -> x2, Pallas kernels: 21.9 us -> 20.9 us  [the longest x1 19.3 us: on_device(): pl.pallas_call(functools.partial(kernel, sizes), out_shape=(pltpu.VMEM((9...]
where the time goes in v2:
time: 21.7 us; the launch traced here: 21.5 us
  Pallas kernels  20.9 us (96%)
  between operations  0.64 us (3%)
    pallas_call x1, Pallas kernels, on_device(): pl.pallas_call(functools.partial(kernel, sizes), out_shape=(pltpu.VMEM((9...  19.3 us
    pallas_call x1, Pallas kernels, on_device(): pl.pallas_call(emit, out_shape=(jax.ShapeDtypeStruct(offset.shape, f32),...  1.54 us

profile of v2, /device:TPU:0, one launch (start us, length us, event | category | flops | bytes accessed | tf_op | source)
XLA Modules:
  0.0 21.5 jit_solution(1018271421733595266)
XLA Ops:
  0.6 19.3 %shard_map.110 = (f32[9,8,8,128]{3,2,1,0:T(8,128)S(1)}, f32[6,3,8,8,128]{4,3,2,1,0:T(8,128)S(1)}, f32[28,64]{1,0:T(8,128)S(1)}) custom-call(f32[3,8,8,128]{3,2,1,0:T(8,128)} %offset_in.1, f32[3,8,8,128]{3,2,1,0:T(8,128)} %velocity_in.1, f32[3,8,8,128]{3,2,1,0:T(8,128)} %spin_in.1, f32[8,8,128]{2,1,0:T(8,128)} %radius_in.1, f32[6,3,8,8,128]{4,3,2,1,0:T(8,128)} %history_in.1, ...), custom_call_target="tpu_custom_call" | custom-call | tf_op jit(solution)/shard_map/pallas_call | solution.py:552
  20.0 1.5 %shard_map.111 = (f32[3,8,8,128]{3,2,1,0:T(8,128)}, f32[3,8,8,128]{3,2,1,0:T(8,128)}, f32[3,8,8,128]{3,2,1,0:T(8,128)}, f32[6,3,8,8,128]{4,3,2,1,0:T(8,128)}, f32[28,1,1,1,64]{4,3,2,1,0:T(1,128)}) custom-call(f32[9,8,8,128]{3,2,1,0:T(8,128)S(1)} %get-tuple-element.8.moved, f32[6,3,8,8,128]{4,3,2,1,0:T(8,128)S(1)} %get-tuple-element.9.springs, ...), custom_call_target="tpu_custom_call" | custom-call | tf_op jit(solution)/shard_map/pallas_call | solution.py:595

commit v3 on v2

--- a/solution.py
+++ b/solution.py
@@ -78,7 +78,7 @@
     sizes,
     offset_in, velocity_in, spin_in, radius_in, history_in, contacts_in, leaving_ref,
     moved, springs_out, arrivals_ref,
-    fields, spin, history, contacts, stay,
+    fields, spin, history, contacts, stay, shears, alive, kept,
     row_lo, row_hi, halo_yp, halo_ym, face, halo_z,
     sum_c, sum_zp, sum_zm, sum_yp, sum_ym, sum_yzp, sum_yzm,
     rows_p, rows_m, cols, back_x, back_yp, back_ym, back_xy, back_z,
@@ -263,6 +263,23 @@
 
     loads[4].wait()
     loads[5].wait()
+
+    def per_direction(x, carry):
+        codes = [contacts[s, x] for s in range(slots)]
+        for number in range(len(forward_dirs)):
+            shear = [zero] * 3
+            live = zero
+            for s in range(slots):
+                hit = codes[s] == number
+                live = jnp.where(hit, 1.0, live)
+                for k in range(3):
+                    shear[k] = jnp.where(hit, history[s, k, x], shear[k])
+            alive[x, number] = live
+            for k in range(3):
+                shears[x, number, k] = shear[k]
+        return carry
+
+    loop(nx, per_direction, 0, 1)
     for number in range(len(reach)):
 
         @pl.when(there(reach[number]))
@@ -277,9 +294,7 @@
 
     def pairs(x, carry):
         own = [fields[c, x] for c in range(10)]
-        codes = [contacts[s, x] for s in range(slots)]
         own_sum = [zero] * 6
-        springs = []
         for number, (dx, dy, dz) in enumerate(forward_dirs):
             at = x + dx
             other = []
@@ -297,13 +312,8 @@
                 elif dz < 0:
                     value = jnp.where(lane == 0, turn_z(rim, -c), turn_z(value, 1))
                 other.append(value)
-            shear = [zero] * 3
-            live = None
-            for s in range(slots):
-                hit = codes[s] == number
-                live = hit if live is None else jnp.logical_or(live, hit)
-                for k in range(3):
-                    shear[k] = jnp.where(hit, history[s, k, x], shear[k])
+            shear = [shears[x, number, k] for k in range(3)]
+            live = alive[x, number]
             apart = [other[k] - own[k] for k in range(3)]
             for k, step in enumerate((dx, dy, dz)):
                 if step:
@@ -324,12 +334,13 @@
             trial = [contact * (stiff_shear * spring[k] + damp_shear * sliding[k]) for k in range(3)]
             scale = lax.rsqrt(jnp.maximum(dot3(trial, trial), shear_floor * shear_floor))
             factor = jnp.minimum(1.0, friction * repulsion * scale)
-            factor = jnp.where(live, factor, 0.0)
-            repulsion = jnp.where(live, repulsion, 0.0)
+            factor = factor * live
+            repulsion = repulsion * live
             tangent = [factor * trial[k] for k in range(3)]
             pair = [tangent[k] - repulsion * normal[k] for k in range(3)]
             terms = pair + cross3(normal, tangent)
-            springs.append([factor * spring[k] for k in range(3)])
+            for k in range(3):
+                kept[x, number, k] = factor * spring[k]
             for c in range(6):
                 own_sum[c] = own_sum[c] + terms[c]
             react = [-terms[c] if c < 3 else terms[c] for c in range(6)]
@@ -344,20 +355,24 @@
                     into[c, at] += react[c]
         for c in range(6):
             sum_c[c, x] += own_sum[c]
+        return carry
+
+    loop(nx, pairs, 0, 2)
+
+    def per_slot(x, carry):
+        codes = [contacts[s, x] for s in range(slots)]
         staying = stay[x]
-        packed = jnp.where(lane // 2 == 9, turn_z(own[9], 18), 0.0)
+        packed = jnp.where(lane // 2 == 9, turn_z(fields[9, x], 18), 0.0)
         for s in range(slots):
             for k in range(3):
                 value = zero
                 for number in range(len(forward_dirs)):
-                    value = jnp.where(codes[s] == number, springs[number][k], value)
+                    value = jnp.where(codes[s] == number, kept[x, number, k], value)
                 springs_out[s, k, x] = value * staying
                 place = 10 + 3 * s + k
                 packed = jnp.where(lane // 2 == place, turn_z(value, 2 * place), packed)
         bottom[x] = packed
         return carry
-
-    loop(nx, pairs, 0, 1)
 
     def split(x, carry):
         face_p, face_m, edge_p, edge_m = carry
@@ -416,6 +431,8 @@
         @pl.when(there(reach[number]))
         def _(number=number):
             returns[number].start()
+
+    loop(nx, per_slot, 0, 1)
 
     for number, delta in enumerate(reach):
 
@@ -564,6 +581,9 @@
             vmem(slots, 3, nx, ny, nz),
             pltpu.VMEM((slots, nx, ny, nz), jnp.int32),
             vmem(nx, ny, nz),
+            vmem(nx, len(forward_dirs), 3, ny, nz),
+            vmem(nx, len(forward_dirs), ny, nz),
+            vmem(nx, len(forward_dirs), 3, ny, nz),
             vmem(nx, 16, nz),
             vmem(nx, 16, nz),
             vmem(nx + 1, 16, nz),

time: 21.7 us -> 20.2 us (0.931)
  Pallas kernels: 20.9 us -> 19.5 us
    pallas_call x1, Pallas kernels: 19.3 us -> 17.9 us  [on_device(): pl.pallas_call(functools.partial(kernel, sizes), out_shape=(pltpu.VMEM((9...]
where the time goes in v3:
time: 20.2 us; the launch traced here: 20.1 us
  Pallas kernels  19.5 us (97%)
  between operations  0.64 us (3%)
    pallas_call x1, Pallas kernels, on_device(): pl.pallas_call(functools.partial(kernel, sizes), out_shape=(pltpu.VMEM((9...  17.9 us
    pallas_call x1, Pallas kernels, on_device(): pl.pallas_call(emit, out_shape=(jax.ShapeDtypeStruct(offset.shape, f32),...  1.54 us

profile of v3, /device:TPU:0, one launch (start us, length us, event | category | flops | bytes accessed | tf_op | source)
XLA Modules:
  0.0 20.1 jit_solution(14348925157412608316)
XLA Ops:
  0.6 17.9 %shard_map.110 = (f32[9,8,8,128]{3,2,1,0:T(8,128)S(1)}, f32[6,3,8,8,128]{4,3,2,1,0:T(8,128)S(1)}, f32[28,64]{1,0:T(8,128)S(1)}) custom-call(f32[3,8,8,128]{3,2,1,0:T(8,128)} %offset_in.1, f32[3,8,8,128]{3,2,1,0:T(8,128)} %velocity_in.1, f32[3,8,8,128]{3,2,1,0:T(8,128)} %spin_in.1, f32[8,8,128]{2,1,0:T(8,128)} %radius_in.1, f32[6,3,8,8,128]{4,3,2,1,0:T(8,128)} %history_in.1, ...), custom_call_target="tpu_custom_call" | custom-call | tf_op jit(solution)/shard_map/pallas_call | solution.py:569
  18.6 1.5 %shard_map.111 = (f32[3,8,8,128]{3,2,1,0:T(8,128)}, f32[3,8,8,128]{3,2,1,0:T(8,128)}, f32[3,8,8,128]{3,2,1,0:T(8,128)}, f32[6,3,8,8,128]{4,3,2,1,0:T(8,128)}, f32[28,1,1,1,64]{4,3,2,1,0:T(1,128)}) custom-call(f32[9,8,8,128]{3,2,1,0:T(8,128)S(1)} %get-tuple-element.8.moved, f32[6,3,8,8,128]{4,3,2,1,0:T(8,128)S(1)} %get-tuple-element.9.springs, ...), custom_call_target="tpu_custom_call" | custom-call | tf_op jit(solution)/shard_map/pallas_call | solution.py:615
